TPU v7x, 32 devices: a whole 2x2x4 slice. The times are simulated.
32 devices in a mesh: inst: 4 (over x, core), shard: 8 (over z, y).
Axes of the slice: x: 2, y: 2, z: 4, core: 2. Of those that a mesh axis runs over, the one named last changes fastest.
Arguments:
- tokens: bfloat16 [2048, 5120], P(('inst', 'shard')), may hold values from -600 to 600
- norm_gain: float32 [5120], P(('inst', 'shard')), may hold values from 0.1 to 1.9
- master_qkv: float32 [5120, 7168], P(('inst', 'shard')), may hold values from -0.078125 to 0.078125
- qkv_bias: float32 [7168], P(('inst', 'shard')), may hold values from -3 to 3
Outputs:
- qkv_out: bfloat16 [32, 512, 896], P(('inst', 'shard'))
All inputs are finite; a program needn't handle non-finite values.
Results may differ from a plain program's by a relative error of at most 0.0062.
Values may be sent and summed in bfloat16 or wider, within the bound.
A program may use at most 64 MiB of HBM per device.

v0:
```python
import functools

import jax
import jax.numpy as jnp
from jax import lax
from jax.experimental import pallas as pl
from jax.experimental.pallas import tpu as pltpu
from jax.sharding import PartitionSpec as P

QHEADS = 40
KVHEADS = 8
HEAD_DIM = 128
TP = 8


EPSILON = 1e-06
MESH = pl.DeviceIdType.MESH
LANES = 128
TOKEN_PIECES = 2


def partner_2(value, axis, distance):
    mask = 2**distance
    pairs = [(source, source ^ mask) for source in range(lax.axis_size(axis))]
    return lax.ppermute(value, axis, pairs)


def rank_columns(matrix):
    query_cols = QHEADS * HEAD_DIM
    pair_cols = KVHEADS * HEAD_DIM
    leading = matrix.shape[:-1]
    query = matrix[..., :query_cols].reshape(leading + (TP, query_cols // TP))
    keys = matrix[..., query_cols : query_cols + pair_cols].reshape(leading + (TP, pair_cols // TP))
    values = matrix[..., query_cols + pair_cols :].reshape(leading + (TP, pair_cols // TP))
    return jnp.concatenate([query, keys, values], axis=-1)


def normalize(tokens, gain):
    floats = tokens.astype(jnp.float32)
    scale = lax.rsqrt(jnp.mean(floats * floats, axis=-1, keepdims=True) + EPSILON)
    return (floats * scale * gain.astype(jnp.float32)).astype(jnp.bfloat16)


def general_device(tokens, norm_gain, master_qkv, qkv_bias):
    shard_count = lax.axis_size("shard")
    local_rows = master_qkv.shape[0]
    rank_width = master_qkv.shape[1] // TP
    gain_full, bias_full = (
        lax.all_gather(norm_gain.astype(jnp.bfloat16), ("inst", "shard"), axis=0, tiled=True),
        lax.all_gather(qkv_bias.astype(jnp.bfloat16), ("inst", "shard"), axis=0, tiled=True),
    )
    normed = normalize(tokens, gain_full)
    shard_pos = lax.axis_index("shard")
    rank_index = shard_pos % TP
    bit_count = TP.bit_length() - 1
    bit_order = list(range(bit_count))
    group_rows = normed
    for bit_pos in bit_order:
        partner = partner_2(group_rows, "shard", bit_pos)
        lower = jnp.bitwise_and(jnp.right_shift(shard_pos, bit_pos), 1) == 0
        group_rows = jnp.where(
            lower,
            jnp.concatenate([group_rows, partner], 0),
            jnp.concatenate([partner, group_rows], 0),
        )
    copies = shard_count // TP
    inst_block = shard_count * local_rows
    rows_low = master_qkv.astype(jnp.bfloat16)
    ranked = jnp.transpose(rank_columns(rows_low), (1, 0, 2))
    spread = jnp.broadcast_to(ranked[None], (copies,) + ranked.shape)
    outgoing = spread.reshape(shard_count, rows_low.shape[0], rank_width)
    arrived = lax.all_to_all(outgoing, "shard", split_axis=0, concat_axis=0, tiled=True).reshape(
        inst_block, rank_width
    )
    product = jnp.dot(
        group_rows,
        lax.all_gather(arrived, "inst", axis=0, tiled=True),
        preferred_element_type=jnp.float32,
    )
    bias_ranks = rank_columns(bias_full)
    bias_mine = lax.dynamic_index_in_dim(bias_ranks, rank_index, 0, keepdims=False)
    result = (product + bias_mine.astype(jnp.float32)).astype(jnp.bfloat16)
    return result[None]


def kernel(
    dims,
    tok_ref,
    gain_ref,
    w_ref,
    bias_ref,
    out_ref,
    tbuf,
    wbuf,
    wsend,
    bbuf,
    scale_ref,
    t_recv,
    t_send,
    w_recv,
    a_send,
    x_send,
    d_send,
    b_recv,
    b_send,
):
    inst_count, shard_count, group = dims
    devices = inst_count * shard_count
    line = shard_count // 2
    inst = lax.axis_index("inst")
    me = lax.axis_index("shard")
    z = me // 2
    y = lax.rem(me, 2)
    flat = inst * shard_count + me
    core_peer = inst + 1 - 2 * lax.rem(inst, 2)
    x_peer = lax.rem(inst + 2, inst_count)
    y_peer = z * 2 + 1 - y
    rows = w_ref.shape[0]
    width = wsend.shape[2]
    pieces = TOKEN_PIECES
    piece_rows = tok_ref.shape[0] // pieces

    def mate(k):
        dy, dz = k % 2, k // 2
        zz = z if dz == 0 else (z + 1 - 2 * lax.rem(z, 2), lax.rem(z + 2, line), line - 1 - z)[dz - 1]
        return zz * 2 + lax.rem(y + dy, 2)

    barrier = pltpu.get_barrier_semaphore()

    @pl.loop(1, devices)
    def _(step):
        there = lax.rem(flat + step, devices)
        pl.semaphore_signal(
            barrier,
            inc=1,
            device_id=(there // shard_count, lax.rem(there, shard_count)),
            device_id_type=MESH,
        )

    for piece in range(pieces):
        tbuf[me * pieces + piece] = tok_ref[piece * piece_rows : (piece + 1) * piece_rows, :]
    bbuf[flat] = bias_ref[...]
    pl.semaphore_wait(barrier, devices - 1)

    def token_copy(block, piece, way, target):
        index = block * pieces + piece
        return pltpu.make_async_remote_copy(
            src_ref=tbuf.at[index],
            dst_ref=tbuf.at[index],
            send_sem=t_send.at[way, index],
            recv_sem=t_recv.at[index],
            device_id=(inst, target),
            device_id_type=MESH,
        )

    def own_token_copy(piece, way, target):
        index = me * pieces + piece
        return pltpu.make_async_remote_copy(
            src_ref=tok_ref.at[pl.ds(piece * piece_rows, piece_rows)],
            dst_ref=tbuf.at[index],
            send_sem=t_send.at[way, index],
            recv_sem=t_recv.at[index],
            device_id=(inst, target),
            device_id_type=MESH,
        )

    def weight_copy(source, target, slot, send_sem):
        return pltpu.make_async_remote_copy(
            src_ref=source,
            dst_ref=wbuf.at[slot],
            send_sem=send_sem,
            recv_sem=w_recv.at[slot],
            device_id=target,
            device_id_type=MESH,
        )

    def all_gather_copy(k):
        there = mate(k)
        return weight_copy(wsend.at[there], (inst, there), flat, a_send.at[k])

    def x_copy(k):
        slot = inst * shard_count + mate(k)
        source = wsend.at[me] if k == 0 else wbuf.at[slot]
        return weight_copy(source, (x_peer, me), slot, x_send.at[k])

    def core_copy(k, owner, side):
        slot = owner * shard_count + mate(k)
        source = wsend.at[me] if k == 0 and side == 0 else wbuf.at[slot]
        return weight_copy(source, (core_peer, me), slot, d_send.at[side, k])

    up = lax.rem(z + 1, line) * 2 + y
    down = lax.rem(z + line - 1, line) * 2 + y

    def each(condition, action):
        pl.when(condition)(action)

    for piece in range(pieces):
        each(z < line - 1, lambda piece=piece: own_token_copy(piece, 0, up).start())
        each(z > 0, lambda piece=piece: own_token_copy(piece, 1, down).start())
        own_token_copy(piece, 2, y_peer).start()
    gain = gain_ref[...].astype(jnp.bfloat16).astype(jnp.float32)
    query = QHEADS * HEAD_DIM // TP
    pair = KVHEADS * HEAD_DIM // TP
    for rank in range(TP):
        starts = (
            (rank * query, 0, query),
            (TP * query + rank * pair, query, pair),
            (TP * (query + pair) + rank * pair, query + pair, pair),
        )
        for source, target, extent in starts:
            part = w_ref[:, source : source + extent].astype(jnp.bfloat16).astype(jnp.float32)
            wsend[rank, :, target : target + extent] = (part * gain).astype(jnp.bfloat16)
    core_copy(0, inst, 0).start()
    x_copy(0).start()
    all_gather_copy(1).start()
    all_gather_copy(2).start()
    all_gather_copy(3).start()

    def bias_copy(step):
        there = lax.rem(flat + step, devices)
        return pltpu.make_async_remote_copy(
            src_ref=bias_ref,
            dst_ref=bbuf.at[flat],
            send_sem=b_send.at[step],
            recv_sem=b_recv.at[flat],
            device_id=(there // shard_count, lax.rem(there, shard_count)),
            device_id_type=MESH,
        )

    @pl.loop(1, devices)
    def _(step):
        bias_copy(step).start()

    wbuf[flat] = wsend[me]

    def wait_block(slot):
        pltpu.make_async_copy(wbuf.at[slot], wbuf.at[slot], w_recv.at[slot]).wait()

    def wait_token(block, piece):
        index = block * pieces + piece
        pltpu.make_async_copy(tbuf.at[index], tbuf.at[index], t_recv.at[index]).wait()

    def relay_token(distance, piece):
        def from_below():
            block = (z - distance) * 2 + y
            wait_token(block, piece)
            each(z < line - 1, lambda: token_copy(block, piece, 0, up).start())
            token_copy(block, piece, 2, y_peer).start()

        def from_above():
            block = (z + distance) * 2 + y
            wait_token(block, piece)
            each(z > 0, lambda: token_copy(block, piece, 1, down).start())
            token_copy(block, piece, 2, y_peer).start()

        each(z >= distance, from_below)
        each(z + distance < line, from_above)

    def relay_weight(k):
        wait_block(inst * shard_count + mate(k))
        x_copy(k).start()
        core_copy(k, inst, 0).start()

    def relay_x(k):
        wait_block(x_peer * shard_count + mate(k))
        core_copy(k, x_peer, 1).start()

    def relay_hop(distance):
        for piece in range(pieces):
            relay_token(distance, piece)

    def scale_of(index):
        values = tbuf[index].astype(jnp.float32)
        mean = jnp.sum(values * values, axis=-1, keepdims=True) * (1.0 / tok_ref.shape[1])
        scale_ref[pl.ds(pl.multiple_of(index * piece_rows, piece_rows), piece_rows), :] = jnp.broadcast_to(
            lax.rsqrt(mean + EPSILON), (piece_rows, LANES)
        )

    relay_hop(1)
    all_gather_copy(4).start()
    all_gather_copy(5).start()
    all_gather_copy(6).start()
    all_gather_copy(7).start()
    relay_x(0)
    relay_weight(1)
    relay_weight(2)
    relay_weight(3)
    relay_hop(2)
    relay_weight(4)
    relay_weight(5)
    relay_hop(3)
    relay_x(1)
    relay_x(2)
    relay_weight(6)
    relay_weight(7)
    relay_x(3)
    relay_x(4)
    relay_x(5)
    relay_x(6)
    relay_x(7)

    for k in range(shard_count):
        wait_block(core_peer * shard_count + mate(k))
        wait_block(lax.rem(core_peer + 2, inst_count) * shard_count + mate(k))
    for block_z in range(line):
        for piece in range(pieces):
            wait_token(block_z * 2 + 1 - y, piece)

    @pl.loop(0, shard_count * pieces)
    def _(index):
        scale_of(index)

    @pl.loop(1, devices)
    def _(step):
        slot = lax.rem(flat + step, devices)
        pltpu.make_async_copy(bbuf.at[slot], bbuf.at[slot], b_recv.at[slot]).wait()

    per_row = LANES // group
    held = bias_ref.shape[0]
    lane = lax.broadcasted_iota(jnp.int32, (1, LANES), 1) // group

    def bias_row(first):
        row = jnp.zeros((1, LANES), jnp.float32)
        for j in range(per_row):
            number = first + j
            row = jnp.where(lane == j, bbuf[number // held, pl.ds(lax.rem(number, held), 1), :], row)
        return row.astype(jnp.bfloat16).astype(jnp.float32)

    tile = 2 * LANES
    depth = devices * rows
    scale = scale_ref[...]
    for start in range(0, width, tile):
        extent = min(tile, width - start)
        product = jnp.dot(
            tbuf[...].reshape(shard_count * pieces * piece_rows, depth),
            wbuf[:, :, start : start + extent].reshape(depth, extent),
            preferred_element_type=jnp.float32,
        )
        for inner in range(0, extent, LANES):
            at = start + inner
            if at < query:
                column = me * query + at
            elif at < query + pair:
                column = TP * query + me * pair + (at - query)
            else:
                column = TP * (query + pair) + me * pair + (at - query - pair)
            out_ref[0, :, at : at + LANES] = (
                product[:, inner : inner + LANES] * scale + bias_row(column // group)
            ).astype(jnp.bfloat16)

    for piece in range(pieces):
        each(z < line - 1, lambda piece=piece: own_token_copy(piece, 0, up).wait_send())
        each(z > 0, lambda piece=piece: own_token_copy(piece, 1, down).wait_send())
        own_token_copy(piece, 2, y_peer).wait_send()
        for distance in range(1, line):

            def below(piece=piece, distance=distance):
                block = (z - distance) * 2 + y
                each(z < line - 1, lambda: token_copy(block, piece, 0, up).wait_send())
                token_copy(block, piece, 2, y_peer).wait_send()

            def above(piece=piece, distance=distance):
                block = (z + distance) * 2 + y
                each(z > 0, lambda: token_copy(block, piece, 1, down).wait_send())
                token_copy(block, piece, 2, y_peer).wait_send()

            each(z >= distance, below)
            each(z + distance < line, above)
    for k in range(shard_count):
        if k:
            all_gather_copy(k).wait_send()
        x_copy(k).wait_send()
        core_copy(k, inst, 0).wait_send()
        core_copy(k, x_peer, 1).wait_send()

    @pl.loop(1, devices)
    def _(step):
        bias_copy(step).wait_send()


def kernel_device(dims, tokens, norm_gain, master_qkv, qkv_bias):
    inst_count, shard_count, group = dims
    devices = inst_count * shard_count
    rows = master_qkv.shape[0]
    width = master_qkv.shape[1] // TP
    pieces = TOKEN_PIECES
    groups = qkv_bias.shape[0] // group
    bias = jnp.tile(qkv_bias.reshape(groups, group), (1, LANES // group))
    index_count = shard_count * pieces
    dma = pltpu.SemaphoreType.DMA
    vmem = pl.BlockSpec(memory_space=pltpu.VMEM)
    return pl.pallas_call(
        functools.partial(kernel, dims),
        out_shape=jax.ShapeDtypeStruct((1, shard_count * tokens.shape[0], width), jnp.bfloat16),
        in_specs=[vmem] * 4,
        out_specs=vmem,
        scratch_shapes=[
            pltpu.VMEM((index_count, tokens.shape[0] // pieces, tokens.shape[1]), jnp.bfloat16),
            pltpu.VMEM((devices, rows, width), jnp.bfloat16),
            pltpu.VMEM((TP, rows, width), jnp.bfloat16),
            pltpu.VMEM((devices, groups, LANES), jnp.float32),
            pltpu.VMEM((shard_count * tokens.shape[0], LANES), jnp.float32),
            dma((index_count,)),
            dma((3, index_count)),
            dma((devices,)),
            dma((shard_count,)),
            dma((shard_count,)),
            dma((2, shard_count)),
            dma((devices,)),
            dma((devices,)),
        ],
        compiler_params=pltpu.CompilerParams(
            collective_id=0, has_side_effects=True, vmem_limit_bytes=60 * 1024 * 1024
        ),
    )(tokens, norm_gain.reshape(rows, 1), master_qkv, bias)


def per_device(tokens, norm_gain, master_qkv, qkv_bias):
    inst_count, shard_count = lax.axis_size("inst"), lax.axis_size("shard")
    group = 32
    fits = (
        shard_count == TP
        and inst_count == 4
        and master_qkv.shape[0] % 16 == 0
        and tokens.shape[0] % (16 * TOKEN_PIECES) == 0
        and qkv_bias.shape[0] % group == 0
    )
    if fits:
        return kernel_device((inst_count, shard_count, group), tokens, norm_gain, master_qkv, qkv_bias)
    return general_device(tokens, norm_gain, master_qkv, qkv_bias)


def solution(mesh):
    in_specs = (
        P(("inst", "shard"), None),
        P(("inst", "shard")),
        P(("inst", "shard"), None),
        P(("inst", "shard")),
    )
    out_specs = P(("inst", "shard"), None, None)
    return jax.shard_map(
        per_device, mesh=mesh, in_specs=in_specs, out_specs=out_specs, check_vma=False
    )
```

profile of v0, /device:TPU:0, one launch (start us, length us, event | category | flops | bytes accessed | tf_op | source)
XLA Modules:
  0.0 121.6 jit_solution(5541677318965233423)
XLA Ops:
  0.0 0.8 tile.10
  0.8 0.7 tile.12.bias_ref
  1.4 1.4 %copy.5.gain_ref = f32[160,1]{1,0:T(8,128)} copy(f32[160,1]{0,1:T(1,128)} %bitcast.1) | data formatting | bytes 1280 | tf_op jit(solution)/shard_map/reshape | solution.py:415
  2.9 116.6 %shard_map.46 = bf16[1,512,896]{2,1,0:T(8,128)(2,1)} custom-call(bf16[64,5120]{1,0:T(8,128)(2,1)} %tok_ref.1, f32[160,1]{1,0:T(8,128)} %copy.5.gain_ref, f32[160,7168]{1,0:T(8,128)} %w_ref.1, f32[7,128]{1,0:T(8,128)} %tile.12.bias_ref), custom_call_target="tpu_custom_call" | custom-call | tf_op jit(solution)/shard_map/pallas_call | solution.py:392
  119.4 2.2 %copy.7 = bf16[1,512,896]{2,1,0:T(8,128)(2,1)} copy(bf16[1,512,896]{2,1,0:T(8,128)(2,1)} %shard_map.46) | data formatting | bytes 1835008
  (1 shorter events, 0.0 us)
where the time goes:
time: 123 us; the launch traced here: 122 us
  Pallas kernels  117 us (95%)
  local copies, waits for them, and re-layouts  5.03 us (4%)
    pallas_call x1, Pallas kernels, kernel_device(): pl.pallas_call(functools.partial(kernel, dims), out_shape=jax.ShapeDtypeS...  117 us

commit v1 on v0

v1 whole, which is shorter than its diff:
```python
import functools

import jax
import jax.numpy as jnp
from jax import lax
from jax.experimental import pallas as pl
from jax.experimental.pallas import tpu as pltpu
from jax.sharding import PartitionSpec as P

QHEADS = 40
KVHEADS = 8
HEAD_DIM = 128
TP = 8


EPSILON = 1e-06
MESH = pl.DeviceIdType.MESH
LANES = 128
TOKEN_PIECES = 2
CHUNKS = ((0, 2), (2, 4), (4, 7))


def partner_2(value, axis, distance):
    mask = 2**distance
    pairs = [(source, source ^ mask) for source in range(lax.axis_size(axis))]
    return lax.ppermute(value, axis, pairs)


def rank_columns(matrix):
    query_cols = QHEADS * HEAD_DIM
    pair_cols = KVHEADS * HEAD_DIM
    leading = matrix.shape[:-1]
    query = matrix[..., :query_cols].reshape(leading + (TP, query_cols // TP))
    keys = matrix[..., query_cols : query_cols + pair_cols].reshape(leading + (TP, pair_cols // TP))
    values = matrix[..., query_cols + pair_cols :].reshape(leading + (TP, pair_cols // TP))
    return jnp.concatenate([query, keys, values], axis=-1)


def normalize(tokens, gain):
    floats = tokens.astype(jnp.float32)
    scale = lax.rsqrt(jnp.mean(floats * floats, axis=-1, keepdims=True) + EPSILON)
    return (floats * scale * gain.astype(jnp.float32)).astype(jnp.bfloat16)


def general_device(tokens, norm_gain, master_qkv, qkv_bias):
    shard_count = lax.axis_size("shard")
    local_rows = master_qkv.shape[0]
    rank_width = master_qkv.shape[1] // TP
    gain_full, bias_full = (
        lax.all_gather(norm_gain.astype(jnp.bfloat16), ("inst", "shard"), axis=0, tiled=True),
        lax.all_gather(qkv_bias.astype(jnp.bfloat16), ("inst", "shard"), axis=0, tiled=True),
    )
    normed = normalize(tokens, gain_full)
    shard_pos = lax.axis_index("shard")
    rank_index = shard_pos % TP
    bit_count = TP.bit_length() - 1
    bit_order = list(range(bit_count))
    group_rows = normed
    for bit_pos in bit_order:
        partner = partner_2(group_rows, "shard", bit_pos)
        lower = jnp.bitwise_and(jnp.right_shift(shard_pos, bit_pos), 1) == 0
        group_rows = jnp.where(
            lower,
            jnp.concatenate([group_rows, partner], 0),
            jnp.concatenate([partner, group_rows], 0),
        )
    copies = shard_count // TP
    inst_block = shard_count * local_rows
    rows_low = master_qkv.astype(jnp.bfloat16)
    ranked = jnp.transpose(rank_columns(rows_low), (1, 0, 2))
    spread = jnp.broadcast_to(ranked[None], (copies,) + ranked.shape)
    outgoing = spread.reshape(shard_count, rows_low.shape[0], rank_width)
    arrived = lax.all_to_all(outgoing, "shard", split_axis=0, concat_axis=0, tiled=True).reshape(
        inst_block, rank_width
    )
    product = jnp.dot(
        group_rows,
        lax.all_gather(arrived, "inst", axis=0, tiled=True),
        preferred_element_type=jnp.float32,
    )
    bias_ranks = rank_columns(bias_full)
    bias_mine = lax.dynamic_index_in_dim(bias_ranks, rank_index, 0, keepdims=False)
    result = (product + bias_mine.astype(jnp.float32)).astype(jnp.bfloat16)
    return result[None]


def kernel(
    dims,
    tok_hbm,
    gain_ref,
    w_hbm,
    bias_ref,
    out_ref,
    tok_ref,
    w_ref,
    xsend,
    xbuf,
    wsend,
    wbuf,
    psend,
    pbuf,
    acc,
    bias_own,
    bbuf,
    load_sem,
    x_recv,
    x_send,
    x_relay,
    w_recv,
    w_send,
    wx_send,
    wc_send,
    p_recv,
    p_send,
    b_recv,
    b_send,
):
    inst_count, shard_count, group = dims
    devices = inst_count * shard_count
    inst = lax.axis_index("inst")
    me = lax.axis_index("shard")
    z = me // 2
    y = lax.rem(me, 2)
    half = z // 2
    flat = inst * shard_count + me
    core_peer = inst + 1 - 2 * lax.rem(inst, 2)
    x_peer = lax.rem(inst + 2, inst_count)
    far_core = lax.rem(core_peer + 2, inst_count)
    z_mate = z + 1 - 2 * lax.rem(z, 2)
    z_pair = lax.rem(z + 2, 4)
    z_near = 2 - half
    z_end = 3 - 3 * half
    inner = z_near + z == 3
    rows = w_ref.shape[0]
    tokens, depth = tok_ref.shape
    tiles = wsend.shape[1]
    half_block = 4 * rows
    pieces = TOKEN_PIECES
    piece_rows = tokens // pieces
    parts = len(CHUNKS)

    token_load = pltpu.make_async_copy(tok_hbm, tok_ref, load_sem.at[0])
    weight_load = pltpu.make_async_copy(w_hbm, w_ref, load_sem.at[1])
    token_load.start()
    weight_load.start()

    barrier = pltpu.get_barrier_semaphore()

    @pl.loop(1, devices)
    def _(step):
        there = lax.rem(flat + step, devices)
        pl.semaphore_signal(
            barrier,
            inc=1,
            device_id=(there // shard_count, lax.rem(there, shard_count)),
            device_id_type=MESH,
        )

    def remote(source, target, send_sem, recv_sem, device):
        return pltpu.make_async_remote_copy(
            src_ref=source,
            dst_ref=target,
            send_sem=send_sem,
            recv_sem=recv_sem,
            device_id=device,
            device_id_type=MESH,
        )

    def each(condition, action):
        pl.when(condition)(action)

    def piece_of(ref, piece):
        return ref.at[pl.ds(piece * piece_rows, piece_rows)]

    def own_x(way, piece):
        which, device, side = (
            (half, z_mate * 2 + y, 0),
            (1 - half, z_near * 2 + y, 0),
            (1 - half, z_pair * 2 + y, 0),
            (half, z * 2 + 1 - y, 1),
        )[way]
        return remote(
            piece_of(xsend.at[which], piece),
            piece_of(xbuf.at[side, z], piece),
            x_send.at[way, piece],
            x_recv.at[side, z, piece],
            (inst, device),
        )

    def relay_x(way, block, piece):
        device, side = ((z_mate * 2 + y, 0), (z * 2 + 1 - y, 1))[way]
        return remote(
            piece_of(xbuf.at[0, block], piece),
            piece_of(xbuf.at[side, block], piece),
            x_relay.at[way, block, piece],
            x_recv.at[side, block, piece],
            (inst, device),
        )

    def place(k):
        dz, dy = k // 2, k % 2
        return (z_mate if dz else z), (1 - y if dy else y)

    def slot_of(owner, k):
        pz, py = place(k)
        return owner * 4 + lax.rem(pz, 2) * 2 + py

    def tiles_of(j):
        first, last = CHUNKS[j % parts]
        return first, last - first, (j // parts) * tiles + first

    def rank_of(k, j):
        pz, py = place(k)
        return (pz if j >= parts else lax.rem(pz + 2, 4)) * 2 + py

    def fresh(k, j):
        first, count, _ = tiles_of(j)
        return wsend.at[rank_of(k, j), pl.ds(first, count)]

    def held(slot, j):
        _, count, first = tiles_of(j)
        return wbuf.at[slot, pl.ds(first, count)]

    def w_copy(k, j):
        pz, py = place(k)
        slot = slot_of(inst, 0)
        return remote(fresh(k, j), held(slot, j), w_send.at[k - 1, j], w_recv.at[slot, j], (inst, pz * 2 + py))

    def wx_copy(k, j):
        slot = slot_of(inst, k)
        source = held(slot, j) if k else fresh(0, j)
        return remote(source, held(slot, j), wx_send.at[k, j], w_recv.at[slot, j], (x_peer, me))

    def wc_copy(side, k, j):
        slot = slot_of((inst, x_peer)[side], k)
        source = held(slot, j) if k or side else fresh(0, j)
        return remote(source, held(slot, j), wc_send.at[side, k, j], w_recv.at[slot, j], (core_peer, me))

    def p_copy(m, j):
        first, count, _ = tiles_of(j)
        return remote(
            psend.at[m, pl.ds(first, count)],
            pbuf.at[m, pl.ds(first, count)],
            p_send.at[m, j],
            p_recv.at[m, j],
            (inst, z_pair * 2 + y),
        )

    def arrived(ref, sem):
        pltpu.make_async_copy(ref, ref, sem).wait()

    def wait_x(side, block, piece):
        arrived(piece_of(xbuf.at[side, block], piece), x_recv.at[side, block, piece])

    def wait_w(slot, j):
        arrived(held(slot, j), w_recv.at[slot, j])

    query = QHEADS * HEAD_DIM // TP
    pair = KVHEADS * HEAD_DIM // TP
    held_bias = bias_ref.shape[1]
    per_row = LANES // group
    groups = held_bias // group

    def needs(owner, rank):
        low, high = owner * held_bias, owner * held_bias + held_bias
        result = None
        for start, extent in (
            (rank * query, query),
            (TP * query + rank * pair, pair),
            (TP * (query + pair) + rank * pair, pair),
        ):
            overlap = jnp.logical_and(start < high, low < start + extent)
            result = overlap if result is None else jnp.logical_or(result, overlap)
        return result

    def bias_copy(step):
        there = lax.rem(flat + step, devices)
        return remote(
            bias_own,
            bbuf.at[flat],
            b_send.at[step],
            b_recv.at[flat],
            (there // shard_count, lax.rem(there, shard_count)),
        )

    def send_bias(finish):
        @pl.loop(1, devices)
        def _(step):
            there = lax.rem(flat + step, devices)

            @pl.when(needs(flat, lax.rem(there, shard_count)))
            def _():
                if finish:
                    bias_copy(step).wait_send()
                else:
                    bias_copy(step).start()

    def bias_row(number_first):
        lane = lax.broadcasted_iota(jnp.int32, (1, LANES), 1) // group
        row = jnp.zeros((1, LANES), jnp.float32)
        for q in range(per_row):
            number = number_first + q
            row = jnp.where(lane == q, bbuf[number // groups, pl.ds(lax.rem(number, groups), 1), :], row)
        return row

    def column_of(t):
        at = t * LANES
        if at < query:
            return me * query + at
        if at < query + pair:
            return TP * query + me * pair + (at - query)
        return TP * (query + pair) + me * pair + (at - query - pair)

    ids = lax.broadcasted_iota(jnp.int32, (rows, rows), 0), lax.broadcasted_iota(jnp.int32, (rows, rows), 1)
    gain_row = gain_ref[...].astype(jnp.bfloat16).astype(jnp.float32)
    gain = jnp.sum(jnp.where(ids[0] == ids[1], jnp.broadcast_to(gain_row, (rows, rows)), 0.0), axis=1, keepdims=True)
    group_id = lax.broadcasted_iota(jnp.int32, (8, held_bias), 0)
    lane_id = lax.broadcasted_iota(jnp.int32, (8, held_bias), 1)
    spread = jnp.where(lane_id // group == group_id, jnp.broadcast_to(bias_ref[...], (8, held_bias)), 0.0)
    from_id = lax.broadcasted_iota(jnp.int32, (held_bias, LANES), 0)
    to_id = lax.broadcasted_iota(jnp.int32, (held_bias, LANES), 1)
    pick = jnp.where(lax.rem(from_id, group) == lax.rem(to_id, group), 1.0, 0.0).astype(jnp.bfloat16)
    bias_own[...] = jnp.dot(spread.astype(jnp.bfloat16), pick, preferred_element_type=jnp.float32)

    token_load.wait()
    step_rows = 16
    for first in range(0, tokens, step_rows):
        values = tok_ref[first : first + step_rows, :].astype(jnp.float32)
        mean = jnp.sum(values * values, axis=-1, keepdims=True) * (1.0 / depth)
        scaled = (values * lax.rsqrt(mean + EPSILON)).astype(jnp.bfloat16)
        for which in range(2):
            for owner in range(inst_count):
                at = (owner * 2 + which) * half_block
                xsend[which, first : first + step_rows, owner * half_block : (owner + 1) * half_block] = scaled[
                    :, at : at + half_block
                ]
    pl.semaphore_wait(barrier, devices - 1)

    for piece in range(pieces):
        own_x(1, piece).start()
        own_x(0, piece).start()
        own_x(3, piece).start()
    xbuf[0, z] = xsend[half]

    weight_load.wait()
    for rank in range(TP):
        starts = (
            (rank * query, 0, query),
            (TP * query + rank * pair, query, pair),
            (TP * (query + pair) + rank * pair, query + pair, pair),
        )
        for source, target, extent in starts:
            for inside in range(0, extent, LANES):
                part = w_ref[:, source + inside : source + inside + LANES].astype(jnp.bfloat16).astype(jnp.float32)
                wsend[rank, (target + inside) // LANES] = (part * gain).astype(jnp.bfloat16)

    def product(m, j):
        first, count, at = tiles_of(j)
        lhs = xbuf[m].reshape(4 * tokens, 4 * half_block)
        result = []
        for t in range(0, count, 2):
            width = min(2, count - t)
            rhs = [wbuf[:, at + t + u].reshape(4 * half_block, LANES) for u in range(width)]
            rhs = jnp.concatenate(rhs, axis=1) if width > 1 else rhs[0]
            value = jnp.dot(lhs, rhs, preferred_element_type=jnp.float32)
            for u in range(width):
                result.append((first + t + u, value[:, u * LANES : (u + 1) * LANES]))
        return result

    def step_wp(j):
        for k in (2, 1, 3):
            w_copy(k, j).start()

    def step_ox(j):
        wx_copy(0, j).start()
        wc_copy(0, 0, j).start()

    def step_rx(block, to_mate):
        for piece in range(pieces):
            wait_x(0, block, piece)
            if to_mate:
                relay_x(0, block, piece).start()
            relay_x(1, block, piece).start()

    def step_rw(j, ks=(2, 1, 3)):
        for k in ks:
            wait_w(slot_of(inst, k), j)
            wx_copy(k, j).start()
            wc_copy(0, k, j).start()

    def step_rc(j, ks=(0, 2, 1, 3)):
        for k in ks:
            wait_w(slot_of(x_peer, k), j)
            wc_copy(1, k, j).start()

    def step_wc(j):
        for k in range(4):
            wait_w(slot_of(core_peer, k), j)
            wait_w(slot_of(far_core, k), j)

    def step_x1():
        for k in range(4):
            for piece in range(pieces):
                wait_x(1, k, piece)

    def step_pm(m, j):
        for t, value in product(m, j):
            psend[m, t] = value.astype(jnp.bfloat16)
        p_copy(m, j).start()

    def step_om(m, j):
        for t, value in product(m, j):
            acc[m, t] = value

    def step_fin(m, j):
        first, count, _ = tiles_of(j)
        arrived(pbuf.at[m, pl.ds(first, count)], p_recv.at[m, j])
        where = 1 - y if m else y
        for t in range(first, first + count):
            value = acc[m, t] + pbuf[m, t].astype(jnp.float32) + bias_row(column_of(t) // group)
            value = value.astype(jnp.bfloat16)
            for k in range(4):
                out_ref[k, where, :, t * LANES : (t + 1) * LANES] = value[k * tokens : (k + 1) * tokens]

    def step_bias():
        send_bias(False)

    def step_bias_wait():
        @pl.loop(1, devices)
        def _(step):
            slot = lax.rem(flat + step, devices)

            @pl.when(needs(slot, me))
            def _():
                arrived(bbuf.at[slot], b_recv.at[slot])

        bbuf[flat] = bias_own[...]

    def run(steps):
        for name, *args in steps:
            names[name](*args)

    names = dict(
        wp=step_wp,
        ox=step_ox,
        rx=step_rx,
        rw=step_rw,
        rc=step_rc,
        wc=step_wc,
        x1=step_x1,
        pm=step_pm,
        om=step_om,
        fin=step_fin,
        bias=step_bias,
        biasw=step_bias_wait,
    )
    first = [("wp", 0), ("ox", 0), ("ox", 1), ("ox", 2)]
    for_inner = [
        ("rx", z_near, True),
        ("rx", z_mate, False),
        ("rx", z_end, True),
        ("wp", 1),
        ("wp", 2),
        ("ox", 3),
        ("ox", 4),
        ("ox", 5),
        ("rw", 0),
        ("wp", 3),
        ("rc", 0),
        ("wc", 0),
        ("pm", 0, 0),
        ("wp", 4),
    ]
    for_outer = [
        ("rx", z_mate, False),
        ("wp", 1),
        ("wp", 2),
        ("ox", 3),
        ("ox", 4),
        ("ox", 5),
        ("rw", 0),
        ("rx", z_near, False),
        ("wp", 3),
        ("rc", 0),
        ("rx", z_end, False),
        ("wp", 4),
        ("wc", 0),
        ("pm", 0, 0),
    ]
    last = [
        ("rw", 1),
        ("rc", 1),
        ("wc", 1),
        ("pm", 0, 1),
        ("wp", 5),
        ("rw", 2),
        ("rc", 2),
        ("wc", 2),
        ("pm", 0, 2),
        ("bias",),
        ("x1",),
        ("pm", 1, 0),
        ("pm", 1, 1),
        ("pm", 1, 2),
        ("biasw",),
        ("rw", 3),
        ("rc", 3),
        ("rw", 4),
        ("rc", 4),
        ("wc", 3),
        ("om", 0, 0 + parts),
        ("om", 1, 0 + parts),
        ("rw", 5),
        ("rc", 5),
        ("wc", 4),
        ("om", 0, 1 + parts),
        ("om", 1, 1 + parts),
        ("wc", 5),
        ("om", 0, 2 + parts),
        ("om", 1, 2 + parts),
        ("fin", 0, 0),
        ("fin", 0, 1),
        ("fin", 0, 2),
        ("fin", 1, 0),
        ("fin", 1, 1),
        ("fin", 1, 2),
    ]
    mine = slot_of(inst, 0)
    run(first)
    wbuf[mine, :tiles] = wsend[rank_of(0, 0)]
    wbuf[mine, tiles:] = wsend[rank_of(0, parts)]
    each(inner, lambda: run(for_inner))
    each(jnp.logical_not(inner), lambda: run(for_outer))
    run(last)

    for piece in range(pieces):
        own_x(0, piece).wait_send()
        own_x(1, piece).wait_send()
        own_x(3, piece).wait_send()
        for block in (z_near, z_mate, z_end):
            relay_x(1, block, piece).wait_send()

        def mate_sends(piece=piece):
            relay_x(0, z_near, piece).wait_send()
            relay_x(0, z_end, piece).wait_send()

        each(inner, mate_sends)
    for j in range(2 * parts):
        for k in range(4):
            if k:
                w_copy(k, j).wait_send()
            wx_copy(k, j).wait_send()
            wc_copy(0, k, j).wait_send()
            wc_copy(1, k, j).wait_send()
    for m in range(2):
        for j in range(parts):
            p_copy(m, j).wait_send()
    send_bias(True)


def kernel_device(dims, tokens, norm_gain, master_qkv, qkv_bias):
    inst_count, shard_count, group = dims
    devices = inst_count * shard_count
    rows = master_qkv.shape[0]
    count, depth = tokens.shape
    tiles = master_qkv.shape[1] // TP // LANES
    pieces = TOKEN_PIECES
    parts = len(CHUNKS)
    dma = pltpu.SemaphoreType.DMA
    vmem = pl.BlockSpec(memory_space=pltpu.VMEM)
    anywhere = pl.BlockSpec(memory_space=pl.ANY)
    low, wide = jnp.bfloat16, jnp.float32
    result = pl.pallas_call(
        functools.partial(kernel, dims),
        out_shape=jax.ShapeDtypeStruct((4, 2, count, tiles * LANES), low),
        in_specs=[anywhere, vmem, anywhere, vmem],
        out_specs=vmem,
        scratch_shapes=[
            pltpu.VMEM((count, depth), low),
            pltpu.VMEM((rows, master_qkv.shape[1]), wide),
            pltpu.VMEM((2, count, depth // 2), low),
            pltpu.VMEM((2, 4, count, depth // 2), low),
            pltpu.VMEM((TP, tiles, rows, LANES), low),
            pltpu.VMEM((4 * inst_count, 2 * tiles, rows, LANES), low),
            pltpu.VMEM((2, tiles, 4 * count, LANES), low),
            pltpu.VMEM((2, tiles, 4 * count, LANES), low),
            pltpu.VMEM((2, tiles, 4 * count, LANES), wide),
            pltpu.VMEM((8, LANES), wide),
            pltpu.VMEM((devices, 8, LANES), wide),
            dma((2,)),
            dma((2, 4, pieces)),
            dma((4, pieces)),
            dma((2, 4, pieces)),
            dma((4 * inst_count, 2 * parts)),
            dma((3, 2 * parts)),
            dma((4, 2 * parts)),
            dma((2, 4, 2 * parts)),
            dma((2, parts)),
            dma((2, parts)),
            dma((devices,)),
            dma((devices,)),
        ],
        compiler_params=pltpu.CompilerParams(
            collective_id=0, has_side_effects=True, vmem_limit_bytes=60 * 1024 * 1024
        ),
    )(tokens, norm_gain.reshape(1, rows), master_qkv, qkv_bias.reshape(1, -1))
    return result.reshape(1, shard_count * count, tiles * LANES)


def per_device(tokens, norm_gain, master_qkv, qkv_bias):
    inst_count, shard_count = lax.axis_size("inst"), lax.axis_size("shard")
    group = 32
    fits = (
        shard_count == TP
        and inst_count == 4
        and master_qkv.shape[0] % 16 == 0
        and tokens.shape[0] % (16 * TOKEN_PIECES) == 0
        and QHEADS * HEAD_DIM // TP % LANES == 0
        and KVHEADS * HEAD_DIM // TP == LANES
        and 4 * master_qkv.shape[0] % LANES == 0
        and qkv_bias.shape[0] % group == 0
    )
    if fits:
        return kernel_device((inst_count, shard_count, group), tokens, norm_gain, master_qkv, qkv_bias)
    return general_device(tokens, norm_gain, master_qkv, qkv_bias)


def solution(mesh):
    in_specs = (
        P(("inst", "shard"), None),
        P(("inst", "shard")),
        P(("inst", "shard"), None),
        P(("inst", "shard")),
    )
    out_specs = P(("inst", "shard"), None, None)
    return jax.shard_map(
        per_device, mesh=mesh, in_specs=in_specs, out_specs=out_specs, check_vma=False
    )
```

time: 123 us -> 126 us (1.024)
  Pallas kernels: 117 us -> 123 us
  local copies, waits for them, and re-layouts: 5.03 us -> 2.18 us
    pallas_call x1, Pallas kernels: 117 us -> 123 us  [kernel_device(): pl.pallas_call(functools.partial(kernel, dims), out_shape=jax.ShapeDtypeS...]
    another operation x3 -> x0, local copies, waits for them, and re-layouts: 1.43 us -> none  [kernel_device(): bias = jnp.tile(qkv_bias.reshape(groups, group), (1, LANES // group))]
    reshape x1 -> x0, local copies, waits for them, and re-layouts: 1.43 us -> none  [kernel_device(): norm_gain.reshape(rows, 1)]
where the time goes in v1:
time: 126 us; the launch traced here: 125 us
  Pallas kernels  123 us (98%)
  local copies, waits for them, and re-layouts  2.18 us (2%)
    pallas_call x1, Pallas kernels, kernel_device(): pl.pallas_call(functools.partial(kernel, dims), out_shape=jax.ShapeDtypeS...  123 us

profile of v1, /device:TPU:0, one launch (start us, length us, event | category | flops | bytes accessed | tf_op | source)
XLA Modules:
  0.0 125.5 jit_solution(13404400743328125023)
XLA Ops:
  0.0 123.3 %shard_map.46 = bf16[4,2,64,896]{3,2,1,0:T(8,128)(2,1)} custom-call(bf16[64,5120]{1,0:T(8,128)(2,1)} %tok_hbm.1, f32[1,160]{1,0:T(1,128)} %bitcast.4, f32[160,7168]{1,0:T(8,128)} %w_hbm.1, f32[1,224]{1,0:T(1,128)} %bitcast.5), custom_call_target="tpu_custom_call" | custom-call | tf_op jit(solution)/shard_map/pallas_call | solution.py:573
  123.3 2.2 %copy.6 = bf16[1,512,896]{2,1,0:T(8,128)(2,1)} copy(bf16[1,512,896]{2,1,0:T(8,128)(2,1)} %bitcast.3) | data formatting | bytes 1835008

commit v2 on v1

--- a/solution.py
+++ b/solution.py
@@ -336,10 +336,10 @@
                 ]
     pl.semaphore_wait(barrier, devices - 1)
 
+    send_bias(False)
     for piece in range(pieces):
         own_x(1, piece).start()
         own_x(0, piece).start()
-        own_x(3, piece).start()
     xbuf[0, z] = xsend[half]
 
     weight_load.wait()
@@ -367,28 +367,35 @@
                 result.append((first + t + u, value[:, u * LANES : (u + 1) * LANES]))
         return result
 
-    def step_wp(j):
-        for k in (2, 1, 3):
+    def step_wp(j, *ks):
+        for k in ks:
             w_copy(k, j).start()
 
     def step_ox(j):
         wx_copy(0, j).start()
         wc_copy(0, 0, j).start()
+
+    def step_xy():
+        for piece in range(pieces):
+            own_x(3, piece).start()
 
     def step_rx(block, to_mate):
         for piece in range(pieces):
             wait_x(0, block, piece)
             if to_mate:
                 relay_x(0, block, piece).start()
+
+    def step_ry(block):
+        for piece in range(pieces):
             relay_x(1, block, piece).start()
 
-    def step_rw(j, ks=(2, 1, 3)):
+    def step_rw(j, *ks):
         for k in ks:
             wait_w(slot_of(inst, k), j)
             wx_copy(k, j).start()
             wc_copy(0, k, j).start()
 
-    def step_rc(j, ks=(0, 2, 1, 3)):
+    def step_rc(j, *ks):
         for k in ks:
             wait_w(slot_of(x_peer, k), j)
             wc_copy(1, k, j).start()
@@ -422,9 +429,6 @@
             for k in range(4):
                 out_ref[k, where, :, t * LANES : (t + 1) * LANES] = value[k * tokens : (k + 1) * tokens]
 
-    def step_bias():
-        send_bias(False)
-
     def step_bias_wait():
         @pl.loop(1, devices)
         def _(step):
@@ -440,10 +444,16 @@
         for name, *args in steps:
             names[name](*args)
 
+    def run(steps):
+        for name, *args in steps:
+            names[name](*args)
+
     names = dict(
         wp=step_wp,
         ox=step_ox,
+        xy=step_xy,
         rx=step_rx,
+        ry=step_ry,
         rw=step_rw,
         rc=step_rc,
         wc=step_wc,
@@ -451,87 +461,115 @@
         pm=step_pm,
         om=step_om,
         fin=step_fin,
-        bias=step_bias,
         biasw=step_bias_wait,
     )
-    first = [("wp", 0), ("ox", 0), ("ox", 1), ("ox", 2)]
+    every = (0, 2, 1, 3)
+    both_first = [
+        ("wp", 0, 2, 3, 1),
+        ("ox", 0),
+        ("ox", 1),
+        ("ox", 2),
+        ("wp", 1, 1),
+        ("wp", 2, 1),
+        ("xy",),
+    ]
     for_inner = [
+        ("wp", 1, 2, 3),
+        ("rw", 0, 1),
+        ("rw", 0, 2, 3),
+        ("rw", 1, 1),
+        ("rw", 2, 1),
         ("rx", z_near, True),
+        ("rx", z_end, True),
+        ("rc", 0, *every),
+        ("wp", 2, 2, 3),
         ("rx", z_mate, False),
-        ("rx", z_end, True),
-        ("wp", 1),
-        ("wp", 2),
+        ("ry", z_near),
+        ("ry", z_end),
+        ("ry", z_mate),
+        ("wc", 0),
+        ("pm", 0, 0),
         ("ox", 3),
+        ("rw", 1, 2, 3),
+        ("wp", 3, 2, 3, 1),
+        ("wp", 4, 2, 3, 1),
+        ("wp", 5, 2, 3, 1),
+        ("rc", 1, *every),
+        ("wc", 1),
+        ("pm", 0, 1),
+        ("rw", 2, 2, 3),
         ("ox", 4),
         ("ox", 5),
-        ("rw", 0),
-        ("wp", 3),
-        ("rc", 0),
+        ("rc", 2, *every),
+        ("wc", 2),
+        ("pm", 0, 2),
+    ]
+    for_outer = [
+        ("wp", 1, 2, 3),
+        ("wp", 2, 2, 3),
+        ("rw", 0, 1),
+        ("rx", z_mate, False),
+        ("ry", z_mate),
+        ("rw", 0, 2, 3),
+        ("rw", 1, 1),
+        ("rw", 2, 1),
+        ("rc", 0, *every),
+        ("rw", 1, 2, 3),
+        ("ox", 3),
+        ("wp", 3, 2, 3, 1),
+        ("wp", 4, 2, 3, 1),
+        ("wp", 5, 2, 3, 1),
+        ("rc", 1, *every),
+        ("rx", z_near, False),
+        ("ry", z_near),
+        ("rx", z_end, False),
+        ("ry", z_end),
         ("wc", 0),
         ("pm", 0, 0),
-        ("wp", 4),
-    ]
-    for_outer = [
-        ("rx", z_mate, False),
-        ("wp", 1),
-        ("wp", 2),
-        ("ox", 3),
+        ("wc", 1),
+        ("pm", 0, 1),
+        ("rw", 2, 2, 3),
         ("ox", 4),
         ("ox", 5),
-        ("rw", 0),
-        ("rx", z_near, False),
-        ("wp", 3),
-        ("rc", 0),
-        ("rx", z_end, False),
-        ("wp", 4),
-        ("wc", 0),
-        ("pm", 0, 0),
-    ]
-    last = [
-        ("rw", 1),
-        ("rc", 1),
-        ("wc", 1),
-        ("pm", 0, 1),
-        ("wp", 5),
-        ("rw", 2),
-        ("rc", 2),
+        ("rc", 2, *every),
         ("wc", 2),
         ("pm", 0, 2),
-        ("bias",),
+    ]
+    both_last = [
+        ("rw", 3, 1, 2, 3),
         ("x1",),
         ("pm", 1, 0),
         ("pm", 1, 1),
         ("pm", 1, 2),
-        ("biasw",),
-        ("rw", 3),
-        ("rc", 3),
-        ("rw", 4),
-        ("rc", 4),
+        ("rc", 3, *every),
+        ("rw", 4, 1, 2, 3),
+        ("rc", 4, *every),
         ("wc", 3),
         ("om", 0, 0 + parts),
         ("om", 1, 0 + parts),
-        ("rw", 5),
-        ("rc", 5),
+        ("rw", 5, 1, 2, 3),
+        ("rc", 5, *every),
         ("wc", 4),
         ("om", 0, 1 + parts),
         ("om", 1, 1 + parts),
+        ("biasw",),
+        ("fin", 0, 0),
+        ("fin", 0, 1),
         ("wc", 5),
         ("om", 0, 2 + parts),
         ("om", 1, 2 + parts),
-        ("fin", 0, 0),
-        ("fin", 0, 1),
         ("fin", 0, 2),
         ("fin", 1, 0),
         ("fin", 1, 1),
         ("fin", 1, 2),
     ]
     mine = slot_of(inst, 0)
-    run(first)
+    run(both_first)
     wbuf[mine, :tiles] = wsend[rank_of(0, 0)]
     wbuf[mine, tiles:] = wsend[rank_of(0, parts)]
     each(inner, lambda: run(for_inner))
     each(jnp.logical_not(inner), lambda: run(for_outer))
-    run(last)
+    run(both_last)
 
     for piece in range(pieces):
         own_x(0, piece).wait_send()

time: 126 us -> 97.8 us (0.78)
  Pallas kernels: 123 us -> 95.5 us
    pallas_call x1, Pallas kernels: 123 us -> 95.5 us  [kernel_device(): pl.pallas_call(functools.partial(kernel, dims), out_shape=jax.ShapeDtypeS...]
where the time goes in v2:
time: 97.8 us; the launch traced here: 97.7 us
  Pallas kernels  95.5 us (98%)
  local copies, waits for them, and re-layouts  2.18 us (2%)
    pallas_call x1, Pallas kernels, kernel_device(): pl.pallas_call(functools.partial(kernel, dims), out_shape=jax.ShapeDtypeS...  95.5 us
    unnamed x1, local copies, waits for them, and re-layouts  2.18 us

profile of v2, /device:TPU:0, one launch (start us, length us, event | category | flops | bytes accessed | tf_op | source)
XLA Modules:
  0.0 97.7 jit_solution(8145750146002085894)
XLA Ops:
  0.0 95.5 %shard_map.46 = bf16[4,2,64,896]{3,2,1,0:T(8,128)(2,1)} custom-call(bf16[64,5120]{1,0:T(8,128)(2,1)} %tok_hbm.1, f32[1,160]{1,0:T(1,128)} %bitcast.4, f32[160,7168]{1,0:T(8,128)} %w_hbm.1, f32[1,224]{1,0:T(1,128)} %bitcast.5), custom_call_target="tpu_custom_call" | custom-call | tf_op jit(solution)/shard_map/pallas_call | solution.py:611
  95.5 2.2 %copy.6 = bf16[1,512,896]{2,1,0:T(8,128)(2,1)} copy(bf16[1,512,896]{2,1,0:T(8,128)(2,1)} %bitcast.3) | data formatting | bytes 1835008

commit v3 on v1

--- a/solution.py
+++ b/solution.py
@@ -17,7 +17,272 @@
 MESH = pl.DeviceIdType.MESH
 LANES = 128
 TOKEN_PIECES = 2
-CHUNKS = ((0, 2), (2, 4), (4, 7))
+CHUNKS = (
+    (("far", 0, 2), ("far", 2, 2), ("far", 4, 3), ("extra", 5, 2), ("own", 0, 2), ("own", 2, 3), ("own", 5, 2)),
+    (("far", 0, 2), ("far", 2, 3), ("own", 0, 2), ("own", 2, 2), ("own", 4, 3)),
+)
+INNER = (
+    ("xm", 1, 0),
+    ("xf", 1, 0),
+    ("xf", 0, 0),
+    ("xy", 1, 0),
+    ("wp", 0, 2),
+    ("wp", 1, 1),
+    ("ox", 0, 0),
+    ("ox", 1, 0),
+    ("ko", 0, 0),
+    ("ox", 6, 0),
+    ("ko", 1, 0),
+    ("wp", 3, 1),
+    ("bias", 0, 0),
+    ("rc", 0, 0),
+    ("ox", 3, 0),
+    ("ko", 6, 0),
+    ("rx", 2, 1),
+    ("wp", 2, 1),
+    ("rc", 1, 0),
+    ("ox", 2, 0),
+    ("ko", 3, 0),
+    ("rc", 6, 0),
+    ("ko", 2, 0),
+    ("rx", 2, 0),
+    ("ry", 2, 0),
+    ("rw", 3, 1),
+    ("wd", 1, 0),
+    ("rc", 3, 0),
+    ("ox", 4, 0),
+    ("kw", 3, 1),
+    ("rd", 1, 0),
+    ("wd", 0, 0),
+    ("rc", 2, 0),
+    ("rw", 1, 1),
+    ("ko", 4, 0),
+    ("rd", 3, 0),
+    ("rc", 3, 1),
+    ("rw", 3, 2),
+    ("kw", 1, 1),
+    ("wp", 1, 2),
+    ("rc", 4, 0),
+    ("kw", 3, 2),
+    ("ry", 3, 0),
+    ("xm", 0, 0),
+    ("wp", 6, 1),
+    ("rw", 0, 2),
+    ("rc", 1, 1),
+    ("kw", 0, 2),
+    ("rw", 1, 2),
+    ("rx", 3, 0),
+    ("rc", 3, 2),
+    ("rw", 3, 3),
+    ("kw", 1, 2),
+    ("wp", 0, 1),
+    ("rc", 0, 2),
+    ("rw", 1, 3),
+    ("kw", 3, 3),
+    ("wp", 4, 1),
+    ("rc", 1, 2),
+    ("ox", 5, 0),
+    ("kw", 1, 3),
+    ("rx", 3, 1),
+    ("ry", 2, 1),
+    ("rc", 3, 3),
+    ("ko", 5, 0),
+    ("ry", 1, 1),
+    ("pm", 0, 3),
+    ("wp", 4, 2),
+    ("rc", 1, 3),
+    ("rw", 4, 1),
+    ("kw", 4, 1),
+    ("pm", 0, 1),
+    ("rw", 2, 2),
+    ("rc", 5, 0),
+    ("rw", 2, 1),
+    ("kw", 2, 2),
+    ("wp", 3, 2),
+    ("rc", 4, 1),
+    ("rd", 5, 0),
+    ("rw", 0, 1),
+    ("kw", 2, 1),
+    ("rc", 2, 2),
+    ("rd", 2, 0),
+    ("rw", 6, 1),
+    ("kw", 0, 1),
+    ("wp", 2, 2),
+    ("rd", 0, 0),
+    ("rc", 2, 1),
+    ("kw", 6, 1),
+    ("rw", 5, 3),
+    ("wd", 3, 0),
+    ("wp", 5, 1),
+    ("rc", 0, 1),
+    ("kw", 5, 3),
+    ("wd", 2, 0),
+    ("rw", 2, 3),
+    ("ry", 3, 1),
+    ("rc", 6, 1),
+    ("wd", 4, 0),
+    ("kw", 2, 3),
+    ("rw", 0, 3),
+    ("xy", 0, 0),
+    ("rc", 5, 3),
+    ("kw", 0, 3),
+    ("rw", 5, 1),
+    ("rc", 2, 3),
+    ("kw", 5, 1),
+    ("ry", 1, 0),
+    ("pm", 0, 2),
+    ("rc", 0, 3),
+    ("pm", 0, 0),
+    ("rc", 5, 1),
+    ("rw", 4, 2),
+    ("kw", 4, 2),
+    ("rw", 5, 2),
+    ("kw", 5, 2),
+    ("pm", 1, 0),
+    ("rc", 4, 2),
+    ("pm", 1, 1),
+    ("rd", 4, 0),
+    ("pm", 1, 2),
+    ("rw", 6, 2),
+    ("kw", 6, 2),
+    ("pm", 1, 3),
+    ("rc", 5, 2),
+    ("rw", 4, 3),
+    ("rd", 6, 0),
+    ("kw", 4, 3),
+    ("om", 0, 5),
+    ("rc", 6, 2),
+    ("om", 1, 5),
+    ("rw", 6, 3),
+    ("rc", 4, 3),
+    ("kw", 6, 3),
+    ("fin", 0, 5),
+    ("fin", 1, 5),
+    ("om", 0, 4),
+    ("om", 1, 4),
+    ("fin", 0, 4),
+    ("fin", 1, 4),
+    ("rc", 6, 3),
+    ("om", 0, 6),
+    ("om", 1, 6),
+    ("fin", 0, 6),
+    ("fin", 1, 6),
+)
+OUTER = (
+    ("xm", 0, 0),
+    ("xy", 1, 0),
+    ("wp", 3, 2),
+    ("wp", 0, 1),
+    ("ox", 2, 0),
+    ("ox", 0, 0),
+    ("ko", 2, 0),
+    ("ox", 3, 0),
+    ("ko", 0, 0),
+    ("wd", 3, 0),
+    ("bias", 0, 0),
+    ("rc", 2, 0),
+    ("ox", 4, 0),
+    ("ko", 3, 0),
+    ("ry", 1, 1),
+    ("wd", 0, 0),
+    ("wp", 1, 1),
+    ("rc", 0, 0),
+    ("ko", 4, 0),
+    ("rw", 0, 2),
+    ("wd", 1, 0),
+    ("rc", 3, 0),
+    ("xf", 0, 0),
+    ("rw", 0, 1),
+    ("kw", 0, 2),
+    ("ry", 2, 1),
+    ("wp", 0, 2),
+    ("rc", 4, 0),
+    ("ox", 1, 0),
+    ("rc", 0, 2),
+    ("ko", 1, 0),
+    ("rw", 1, 1),
+    ("ry", 2, 0),
+    ("wp", 1, 2),
+    ("rc", 0, 1),
+    ("kw", 0, 1),
+    ("kw", 1, 1),
+    ("xf", 1, 0),
+    ("rd", 1, 0),
+    ("rc", 1, 0),
+    ("xm", 1, 0),
+    ("rd", 0, 0),
+    ("rc", 1, 1),
+    ("rw", 1, 2),
+    ("kw", 1, 2),
+    ("wp", 2, 2),
+    ("xy", 0, 0),
+    ("rw", 1, 3),
+    ("kw", 1, 3),
+    ("ry", 1, 0),
+    ("rw", 0, 3),
+    ("wd", 5, 0),
+    ("rc", 1, 2),
+    ("kw", 0, 3),
+    ("wd", 2, 0),
+    ("rc", 1, 3),
+    ("ry", 3, 0),
+    ("rc", 0, 3),
+    ("ry", 3, 1),
+    ("pm", 0, 0),
+    ("pm", 0, 1),
+    ("wp", 2, 1),
+    ("rw", 4, 2),
+    ("kw", 4, 2),
+    ("wp", 4, 1),
+    ("pm", 1, 0),
+    ("wp", 3, 1),
+    ("rw", 3, 2),
+    ("pm", 1, 1),
+    ("kw", 3, 2),
+    ("rw", 2, 1),
+    ("rc", 4, 2),
+    ("rw", 2, 2),
+    ("kw", 2, 1),
+    ("rd", 3, 0),
+    ("rc", 3, 2),
+    ("kw", 2, 2),
+    ("rw", 4, 1),
+    ("wp", 4, 2),
+    ("rd", 2, 0),
+    ("rc", 2, 1),
+    ("kw", 4, 1),
+    ("rw", 3, 1),
+    ("rc", 2, 2),
+    ("rd", 4, 0),
+    ("kw", 3, 1),
+    ("wp", 5, 2),
+    ("rw", 2, 3),
+    ("rc", 4, 1),
+    ("rw", 3, 3),
+    ("kw", 2, 3),
+    ("wd", 4, 0),
+    ("rc", 3, 1),
+    ("kw", 3, 3),
+    ("rw", 4, 3),
+    ("wp", 6, 2),
+    ("rc", 2, 3),
+    ("kw", 4, 3),
+    ("om", 0, 2),
+    ("wd", 6, 0),
+    ("rc", 3, 3),
+    ("om", 1, 2),
+    ("om", 0, 3),
+    ("om", 1, 3),
+    ("rc", 4, 3),
+    ("fin", 0, 3),
+    ("fin", 0, 2),
+    ("om", 0, 4),
+    ("om", 1, 4),
+    ("fin", 0, 4),
+    ("fin", 1, 2),
+    ("fin", 1, 4),
+    ("fin", 1, 3),
+)
 
 
 def partner_2(value, axis, distance):
@@ -84,6 +349,11 @@
     return result[None]
 
 
+def chunk_of(kind, j):
+    what, first, count = CHUNKS[kind][j]
+    return what, first, count, sum(c[2] for c in CHUNKS[kind][:j])
+
+
 def kernel(
     dims,
     tok_hbm,
@@ -97,6 +367,7 @@
     xbuf,
     wsend,
     wbuf,
+    dbuf,
     psend,
     pbuf,
     acc,
@@ -104,12 +375,13 @@
     bbuf,
     load_sem,
     x_recv,
+    x1_recv,
     x_send,
-    x_relay,
     w_recv,
+    wx_recv,
+    wc_recv,
+    d_recv,
     w_send,
-    wx_send,
-    wc_send,
     p_recv,
     p_send,
     b_recv,
@@ -125,7 +397,6 @@
     flat = inst * shard_count + me
     core_peer = inst + 1 - 2 * lax.rem(inst, 2)
     x_peer = lax.rem(inst + 2, inst_count)
-    far_core = lax.rem(core_peer + 2, inst_count)
     z_mate = z + 1 - 2 * lax.rem(z, 2)
     z_pair = lax.rem(z + 2, 4)
     z_near = 2 - half
@@ -137,7 +408,6 @@
     half_block = 4 * rows
     pieces = TOKEN_PIECES
     piece_rows = tokens // pieces
-    parts = len(CHUNKS)
 
     token_load = pltpu.make_async_copy(tok_hbm, tok_ref, load_sem.at[0])
     weight_load = pltpu.make_async_copy(w_hbm, w_ref, load_sem.at[1])
@@ -172,18 +442,12 @@
     def piece_of(ref, piece):
         return ref.at[pl.ds(piece * piece_rows, piece_rows)]
 
-    def own_x(way, piece):
-        which, device, side = (
-            (half, z_mate * 2 + y, 0),
-            (1 - half, z_near * 2 + y, 0),
-            (1 - half, z_pair * 2 + y, 0),
-            (half, z * 2 + 1 - y, 1),
-        )[way]
+    def own_x(which, device, side, piece):
         return remote(
             piece_of(xsend.at[which], piece),
             piece_of(xbuf.at[side, z], piece),
-            x_send.at[way, piece],
-            x_recv.at[side, z, piece],
+            x_send.at[0],
+            x1_recv if side else x_recv.at[z, piece],
             (inst, device),
         )
 
@@ -192,68 +456,25 @@
         return remote(
             piece_of(xbuf.at[0, block], piece),
             piece_of(xbuf.at[side, block], piece),
-            x_relay.at[way, block, piece],
-            x_recv.at[side, block, piece],
+            x_send.at[1 + way],
+            x1_recv if side else x_recv.at[block, piece],
             (inst, device),
         )
 
-    def place(k):
-        dz, dy = k // 2, k % 2
-        return (z_mate if dz else z), (1 - y if dy else y)
-
     def slot_of(owner, k):
-        pz, py = place(k)
-        return owner * 4 + lax.rem(pz, 2) * 2 + py
-
-    def tiles_of(j):
-        first, last = CHUNKS[j % parts]
-        return first, last - first, (j // parts) * tiles + first
-
-    def rank_of(k, j):
-        pz, py = place(k)
-        return (pz if j >= parts else lax.rem(pz + 2, 4)) * 2 + py
-
-    def fresh(k, j):
-        first, count, _ = tiles_of(j)
-        return wsend.at[rank_of(k, j), pl.ds(first, count)]
-
-    def held(slot, j):
-        _, count, first = tiles_of(j)
-        return wbuf.at[slot, pl.ds(first, count)]
-
-    def w_copy(k, j):
-        pz, py = place(k)
-        slot = slot_of(inst, 0)
-        return remote(fresh(k, j), held(slot, j), w_send.at[k - 1, j], w_recv.at[slot, j], (inst, pz * 2 + py))
-
-    def wx_copy(k, j):
-        slot = slot_of(inst, k)
-        source = held(slot, j) if k else fresh(0, j)
-        return remote(source, held(slot, j), wx_send.at[k, j], w_recv.at[slot, j], (x_peer, me))
-
-    def wc_copy(side, k, j):
-        slot = slot_of((inst, x_peer)[side], k)
-        source = held(slot, j) if k or side else fresh(0, j)
-        return remote(source, held(slot, j), wc_send.at[side, k, j], w_recv.at[slot, j], (core_peer, me))
-
-    def p_copy(m, j):
-        first, count, _ = tiles_of(j)
-        return remote(
-            psend.at[m, pl.ds(first, count)],
-            pbuf.at[m, pl.ds(first, count)],
-            p_send.at[m, j],
-            p_recv.at[m, j],
-            (inst, z_pair * 2 + y),
-        )
+        return owner * 4 + lax.rem(z_mate if k // 2 else z, 2) * 2 + (1 - y if k % 2 else y)
+
+    def fresh(kind, there, j, side):
+        what, first, count, _ = chunk_of(kind, j)
+        rank = {"far": lax.rem(there + 2, 4), "extra": z_near, "own": there}[what] * 2 + side
+        return wsend.at[rank, pl.ds(first, count)]
+
+    def held(kind, slot, j):
+        _, _, count, at = chunk_of(kind, j)
+        return wbuf.at[slot, pl.ds(at, count)]
 
     def arrived(ref, sem):
         pltpu.make_async_copy(ref, ref, sem).wait()
-
-    def wait_x(side, block, piece):
-        arrived(piece_of(xbuf.at[side, block], piece), x_recv.at[side, block, piece])
-
-    def wait_w(slot, j):
-        arrived(held(slot, j), w_recv.at[slot, j])
 
     query = QHEADS * HEAD_DIM // TP
     pair = KVHEADS * HEAD_DIM // TP
@@ -336,10 +557,22 @@
                 ]
     pl.semaphore_wait(barrier, devices - 1)
 
-    for piece in range(pieces):
-        own_x(1, piece).start()
-        own_x(0, piece).start()
-        own_x(3, piece).start()
+    def send_x(name, piece):
+        which, device, side = {
+            "xf": (1 - half, z_near * 2 + y, 0),
+            "xm": (half, z_mate * 2 + y, 0),
+            "xy": (half, z * 2 + 1 - y, 1),
+        }[name]
+        own_x(which, device, side, piece).start()
+
+    def early(steps):
+        for name, piece, _ in steps:
+            if name not in ("xf", "xm", "xy"):
+                break
+            send_x(name, piece)
+
+    each(inner, lambda: early(INNER))
+    each(jnp.logical_not(inner), lambda: early(OUTER))
     xbuf[0, z] = xsend[half]
 
     weight_load.wait()
@@ -354,8 +587,8 @@
                 part = w_ref[:, source + inside : source + inside + LANES].astype(jnp.bfloat16).astype(jnp.float32)
                 wsend[rank, (target + inside) // LANES] = (part * gain).astype(jnp.bfloat16)
 
-    def product(m, j):
-        first, count, at = tiles_of(j)
+    def product(kind, m, j):
+        _, first, count, at = chunk_of(kind, j)
         lhs = xbuf[m].reshape(4 * tokens, 4 * half_block)
         result = []
         for t in range(0, count, 2):
@@ -364,68 +597,10 @@
             rhs = jnp.concatenate(rhs, axis=1) if width > 1 else rhs[0]
             value = jnp.dot(lhs, rhs, preferred_element_type=jnp.float32)
             for u in range(width):
-                result.append((first + t + u, value[:, u * LANES : (u + 1) * LANES]))
+                result.append((t + u, value[:, u * LANES : (u + 1) * LANES]))
         return result
 
-    def step_wp(j):
-        for k in (2, 1, 3):
-            w_copy(k, j).start()
-
-    def step_ox(j):
-        wx_copy(0, j).start()
-        wc_copy(0, 0, j).start()
-
-    def step_rx(block, to_mate):
-        for piece in range(pieces):
-            wait_x(0, block, piece)
-            if to_mate:
-                relay_x(0, block, piece).start()
-            relay_x(1, block, piece).start()
-
-    def step_rw(j, ks=(2, 1, 3)):
-        for k in ks:
-            wait_w(slot_of(inst, k), j)
-            wx_copy(k, j).start()
-            wc_copy(0, k, j).start()
-
-    def step_rc(j, ks=(0, 2, 1, 3)):
-        for k in ks:
-            wait_w(slot_of(x_peer, k), j)
-            wc_copy(1, k, j).start()
-
-    def step_wc(j):
-        for k in range(4):
-            wait_w(slot_of(core_peer, k), j)
-            wait_w(slot_of(far_core, k), j)
-
-    def step_x1():
-        for k in range(4):
-            for piece in range(pieces):
-                wait_x(1, k, piece)
-
-    def step_pm(m, j):
-        for t, value in product(m, j):
-            psend[m, t] = value.astype(jnp.bfloat16)
-        p_copy(m, j).start()
-
-    def step_om(m, j):
-        for t, value in product(m, j):
-            acc[m, t] = value
-
-    def step_fin(m, j):
-        first, count, _ = tiles_of(j)
-        arrived(pbuf.at[m, pl.ds(first, count)], p_recv.at[m, j])
-        where = 1 - y if m else y
-        for t in range(first, first + count):
-            value = acc[m, t] + pbuf[m, t].astype(jnp.float32) + bias_row(column_of(t) // group)
-            value = value.astype(jnp.bfloat16)
-            for k in range(4):
-                out_ref[k, where, :, t * LANES : (t + 1) * LANES] = value[k * tokens : (k + 1) * tokens]
-
-    def step_bias():
-        send_bias(False)
-
-    def step_bias_wait():
+    def finish_bias():
         @pl.loop(1, devices)
         def _(step):
             slot = lax.rem(flat + step, devices)
@@ -435,127 +610,182 @@
                 arrived(bbuf.at[slot], b_recv.at[slot])
 
         bbuf[flat] = bias_own[...]
-
-    def run(steps):
-        for name, *args in steps:
-            names[name](*args)
-
-    names = dict(
-        wp=step_wp,
-        ox=step_ox,
-        rx=step_rx,
-        rw=step_rw,
-        rc=step_rc,
-        wc=step_wc,
-        x1=step_x1,
-        pm=step_pm,
-        om=step_om,
-        fin=step_fin,
-        bias=step_bias,
-        biasw=step_bias_wait,
-    )
-    first = [("wp", 0), ("ox", 0), ("ox", 1), ("ox", 2)]
-    for_inner = [
-        ("rx", z_near, True),
-        ("rx", z_mate, False),
-        ("rx", z_end, True),
-        ("wp", 1),
-        ("wp", 2),
-        ("ox", 3),
-        ("ox", 4),
-        ("ox", 5),
-        ("rw", 0),
-        ("wp", 3),
-        ("rc", 0),
-        ("wc", 0),
-        ("pm", 0, 0),
-        ("wp", 4),
-    ]
-    for_outer = [
-        ("rx", z_mate, False),
-        ("wp", 1),
-        ("wp", 2),
-        ("ox", 3),
-        ("ox", 4),
-        ("ox", 5),
-        ("rw", 0),
-        ("rx", z_near, False),
-        ("wp", 3),
-        ("rc", 0),
-        ("rx", z_end, False),
-        ("wp", 4),
-        ("wc", 0),
-        ("pm", 0, 0),
-    ]
-    last = [
-        ("rw", 1),
-        ("rc", 1),
-        ("wc", 1),
-        ("pm", 0, 1),
-        ("wp", 5),
-        ("rw", 2),
-        ("rc", 2),
-        ("wc", 2),
-        ("pm", 0, 2),
-        ("bias",),
-        ("x1",),
-        ("pm", 1, 0),
-        ("pm", 1, 1),
-        ("pm", 1, 2),
-        ("biasw",),
-        ("rw", 3),
-        ("rc", 3),
-        ("rw", 4),
-        ("rc", 4),
-        ("wc", 3),
-        ("om", 0, 0 + parts),
-        ("om", 1, 0 + parts),
-        ("rw", 5),
-        ("rc", 5),
-        ("wc", 4),
-        ("om", 0, 1 + parts),
-        ("om", 1, 1 + parts),
-        ("wc", 5),
-        ("om", 0, 2 + parts),
-        ("om", 1, 2 + parts),
-        ("fin", 0, 0),
-        ("fin", 0, 1),
-        ("fin", 0, 2),
-        ("fin", 1, 0),
-        ("fin", 1, 1),
-        ("fin", 1, 2),
-    ]
-    mine = slot_of(inst, 0)
-    run(first)
-    wbuf[mine, :tiles] = wsend[rank_of(0, 0)]
-    wbuf[mine, tiles:] = wsend[rank_of(0, parts)]
-    each(inner, lambda: run(for_inner))
-    each(jnp.logical_not(inner), lambda: run(for_outer))
-    run(last)
-
-    for piece in range(pieces):
-        own_x(0, piece).wait_send()
-        own_x(1, piece).wait_send()
-        own_x(3, piece).wait_send()
-        for block in (z_near, z_mate, z_end):
-            relay_x(1, block, piece).wait_send()
-
-        def mate_sends(piece=piece):
-            relay_x(0, z_near, piece).wait_send()
-            relay_x(0, z_end, piece).wait_send()
-
-        each(inner, mate_sends)
-    for j in range(2 * parts):
-        for k in range(4):
-            if k:
-                w_copy(k, j).wait_send()
-            wx_copy(k, j).wait_send()
-            wc_copy(0, k, j).wait_send()
-            wc_copy(1, k, j).wait_send()
-    for m in range(2):
-        for j in range(parts):
-            p_copy(m, j).wait_send()
-    send_bias(True)
+        send_bias(True)
+
+    def run(kind, steps):
+        other = 1 - kind
+        done = set()
+
+        def once(key, action):
+            if key not in done:
+                done.add(key)
+                action()
+
+        def need_x(block):
+            for piece in range(pieces):
+                once(
+                    ("x", block, piece),
+                    lambda piece=piece: arrived(
+                        piece_of(xbuf.at[0, places[block]], piece), x_recv.at[places[block], piece]
+                    ),
+                )
+
+        def need_w(k, j):
+            once(("w", k, j), lambda: arrived(held(kind, slot_of(inst, k), j), w_recv.at[k - 1, j]))
+
+        def need_chunk(j):
+            _, first, count, at = chunk_of(kind, j)
+
+            def action():
+                arrived(wbuf.at[pl.ds(0, 8), pl.ds(at, count)], wc_recv.at[j])
+                wbuf[slot_of(inst, 0), at : at + count] = fresh(kind, z, j, y)[...]
+
+            once(("c", j), action)
+
+        def need_tokens(m):
+            for block in (1, 2, 3):
+                need_x(block)
+            if m:
+                once("x1", lambda: arrived(xbuf.at[1], x1_recv))
+
+        places = (z, z_mate, z_near, z_end)
+
+        def step_rx(block, piece):
+            once(
+                ("x", block, piece),
+                lambda: arrived(piece_of(xbuf.at[0, places[block]], piece), x_recv.at[places[block], piece]),
+            )
+            relay_x(0, places[block], piece).start()
+
+        def step_ry(block, piece):
+            once(
+                ("x", block, piece),
+                lambda: arrived(piece_of(xbuf.at[0, places[block]], piece), x_recv.at[places[block], piece]),
+            )
+            relay_x(1, places[block], piece).start()
+
+        def step_wp(j, k):
+            mine = slot_of(inst, 0)
+            if k == 1:
+                source, target, device = fresh(kind, z, j, 1 - y), held(kind, mine, j), z * 2 + 1 - y
+            else:
+                source, target, device = fresh(other, z_mate, j, y), held(other, mine, j), z_mate * 2 + y
+            remote(source, target, w_send.at[k - 1], w_recv.at[k - 1, j], (inst, device)).start()
+
+        def step_wd(j, _):
+            _, _, count, at = chunk_of(other, j)
+            target = dbuf.at[pl.ds(at, count)]
+            remote(
+                fresh(other, z_mate, j, 1 - y), target, w_send.at[2], d_recv.at[j], (inst, z_mate * 2 + y)
+            ).start()
+
+        def step_rd(j, _):
+            _, _, count, at = chunk_of(kind, j)
+            source = dbuf.at[pl.ds(at, count)]
+            arrived(source, d_recv.at[j])
+            target = held(kind, slot_of(inst, 2), j)
+            remote(source, target, w_send.at[3], w_recv.at[2, j], (inst, z * 2 + 1 - y)).start()
+
+        def send_block(j, k, source, across):
+            device, send, recv = (
+                ((x_peer, me), w_send.at[4], wx_recv.at[k, j]),
+                ((core_peer, me), w_send.at[5], wc_recv.at[j]),
+            )[across]
+            remote(source, held(kind, slot_of(inst, k), j), send, recv, device).start()
+
+        def step_ox(j, _):
+            send_block(j, 0, fresh(kind, z, j, y), 0)
+
+        def step_ko(j, _):
+            send_block(j, 0, fresh(kind, z, j, y), 1)
+
+        def step_rw(j, k):
+            need_w(k, j)
+            send_block(j, k, held(kind, slot_of(inst, k), j), 0)
+
+        def step_kw(j, k):
+            need_w(k, j)
+            send_block(j, k, held(kind, slot_of(inst, k), j), 1)
+
+        def step_rc(j, k):
+            block = held(kind, slot_of(x_peer, k), j)
+            arrived(block, wx_recv.at[k, j])
+            remote(block, block, w_send.at[5], wc_recv.at[j], (core_peer, me)).start()
+
+        def step_pm(m, j):
+            need_tokens(m)
+            need_chunk(j)
+            what, first, count, at = chunk_of(kind, j)
+            for t, value in product(kind, m, j):
+                psend[m, at + t] = value.astype(jnp.bfloat16)
+            target = other if what == "far" else kind
+            index = [c[:3] for c in CHUNKS[target]].index(("own", first, count))
+            remote(
+                psend.at[m, pl.ds(at, count)],
+                pbuf.at[m, pl.ds(first, count)],
+                p_send.at[0],
+                p_recv.at[m, index],
+                (inst, (z_pair if what == "far" else z_near) * 2 + y),
+            ).start()
+
+        def step_om(m, j):
+            need_tokens(m)
+            need_chunk(j)
+            first = chunk_of(kind, j)[1]
+            for t, value in product(kind, m, j):
+                acc[m, first + t] = value
+
+        def step_fin(m, j):
+            once("bias", finish_bias)
+            _, first, count, _ = chunk_of(kind, j)
+            arrived(pbuf.at[m, pl.ds(first, count)], p_recv.at[m, j])
+            where = 1 - y if m else y
+            for t in range(first, first + count):
+                value = acc[m, t] + pbuf[m, t].astype(jnp.float32) + bias_row(column_of(t) // group)
+                value = value.astype(jnp.bfloat16)
+                for k in range(4):
+                    out_ref[k, where, :, t * LANES : (t + 1) * LANES] = value[k * tokens : (k + 1) * tokens]
+
+        def step_bias(*_):
+            send_bias(False)
+
+        table = dict(
+            xy=lambda piece, _: send_x("xy", piece),
+            xf=lambda piece, _: send_x("xf", piece),
+            xm=lambda piece, _: send_x("xm", piece),
+            rx=step_rx,
+            ry=step_ry,
+            wp=step_wp,
+            wd=step_wd,
+            rd=step_rd,
+            ox=step_ox,
+            ko=step_ko,
+            rw=step_rw,
+            kw=step_kw,
+            rc=step_rc,
+            pm=step_pm,
+            om=step_om,
+            fin=step_fin,
+            bias=step_bias,
+        )
+        start = next(i for i, step in enumerate(steps) if step[0] not in ("xf", "xm", "xy"))
+        for name, first, second in steps[start:]:
+            table[name](first, second)
+
+        counts = [sum(c[2] for c in CHUNKS[way]) for way in range(2)]
+        sent = counts[kind] - tiles
+        once("sent_x", lambda: arrived(xbuf.at[0, pl.ds(0, 3)], x_send.at[0]))
+        once("sent_y", lambda: arrived(xbuf.at[0, pl.ds(0, 3)], x_send.at[2]))
+        if kind == 0:
+            arrived(xbuf.at[0, pl.ds(0, 2)], x_send.at[1])
+        for way, target in enumerate((kind, other, other, kind)):
+            arrived(wbuf.at[0, pl.ds(0, counts[target])], w_send.at[way])
+        arrived(wbuf.at[pl.ds(0, 4), pl.ds(0, counts[kind])], w_send.at[4])
+        arrived(wbuf.at[pl.ds(0, 8), pl.ds(0, counts[kind])], w_send.at[5])
+        arrived(psend.at[:, pl.ds(0, sent)], p_send.at[0])
+
+    each(inner, lambda: run(0, INNER))
+    each(jnp.logical_not(inner), lambda: run(1, OUTER))
 
 
 def kernel_device(dims, tokens, norm_gain, master_qkv, qkv_bias):
@@ -565,7 +795,8 @@
     count, depth = tokens.shape
     tiles = master_qkv.shape[1] // TP // LANES
     pieces = TOKEN_PIECES
-    parts = len(CHUNKS)
+    most = max(len(c) for c in CHUNKS)
+    held = max(sum(c[2] for c in way) for way in CHUNKS)
     dma = pltpu.SemaphoreType.DMA
     vmem = pl.BlockSpec(memory_space=pltpu.VMEM)
     anywhere = pl.BlockSpec(memory_space=pl.ANY)
@@ -581,22 +812,24 @@
             pltpu.VMEM((2, count, depth // 2), low),
             pltpu.VMEM((2, 4, count, depth // 2), low),
             pltpu.VMEM((TP, tiles, rows, LANES), low),
-            pltpu.VMEM((4 * inst_count, 2 * tiles, rows, LANES), low),
-            pltpu.VMEM((2, tiles, 4 * count, LANES), low),
+            pltpu.VMEM((4 * inst_count, held, rows, LANES), low),
+            pltpu.VMEM((held, rows, LANES), low),
+            pltpu.VMEM((2, held - tiles, 4 * count, LANES), low),
             pltpu.VMEM((2, tiles, 4 * count, LANES), low),
             pltpu.VMEM((2, tiles, 4 * count, LANES), wide),
             pltpu.VMEM((8, LANES), wide),
             pltpu.VMEM((devices, 8, LANES), wide),
             dma((2,)),
-            dma((2, 4, pieces)),
             dma((4, pieces)),
-            dma((2, 4, pieces)),
-            dma((4 * inst_count, 2 * parts)),
-            dma((3, 2 * parts)),
-            dma((4, 2 * parts)),
-            dma((2, 4, 2 * parts)),
-            dma((2, parts)),
-            dma((2, parts)),
+            dma,
+            dma((3,)),
+            dma((3, most)),
+            dma((4, most)),
+            dma((most,)),
+            dma((most,)),
+            dma((6,)),
+            dma((2, most)),
+            dma((1,)),
             dma((devices,)),
             dma((devices,)),
         ],

time: 126 us -> 80.5 us (0.64)
  Pallas kernels: 123 us -> 77.8 us
    pallas_call x1, Pallas kernels: 123 us -> 77.8 us  [kernel_device(): pl.pallas_call(functools.partial(kernel, dims), out_shape=jax.ShapeDtypeS...]
where the time goes in v3:
time: 80.5 us; the launch traced here: 80 us
  Pallas kernels  77.8 us (97%)
  local copies, waits for them, and re-layouts  2.18 us (3%)
    pallas_call x1, Pallas kernels, kernel_device(): pl.pallas_call(functools.partial(kernel, dims), out_shape=jax.ShapeDtypeS...  77.8 us
    unnamed x1, local copies, waits for them, and re-layouts  2.18 us

profile of v3, /device:TPU:0, one launch (start us, length us, event | category | flops | bytes accessed | tf_op | source)
XLA Modules:
  0.0 80.0 jit_solution(5742126434216922387)
XLA Ops:
  0.0 77.8 %shard_map.46 = bf16[4,2,64,896]{3,2,1,0:T(8,128)(2,1)} custom-call(bf16[64,5120]{1,0:T(8,128)(2,1)} %tok_hbm.1, f32[1,160]{1,0:T(1,128)} %bitcast.4, f32[160,7168]{1,0:T(8,128)} %w_hbm.1, f32[1,224]{1,0:T(1,128)} %bitcast.5), custom_call_target="tpu_custom_call" | custom-call | tf_op jit(solution)/shard_map/pallas_call | solution.py:804
  77.8 2.2 %copy.6 = bf16[1,512,896]{2,1,0:T(8,128)(2,1)} copy(bf16[1,512,896]{2,1,0:T(8,128)(2,1)} %bitcast.3) | data formatting | bytes 1835008

commit v4 on v3

--- a/solution.py
+++ b/solution.py
@@ -18,270 +18,315 @@
 LANES = 128
 TOKEN_PIECES = 2
 CHUNKS = (
-    (("far", 0, 2), ("far", 2, 2), ("far", 4, 3), ("extra", 5, 2), ("own", 0, 2), ("own", 2, 3), ("own", 5, 2)),
-    (("far", 0, 2), ("far", 2, 3), ("own", 0, 2), ("own", 2, 2), ("own", 4, 3)),
+    (("far", 0, 1), ("far", 1, 2), ("far", 3, 2), ("far", 5, 2), ("extra", 4, 3), ("own", 0, 2), ("own", 2, 2), ("own", 4, 3)),
+    (("far", 0, 2), ("far", 2, 2), ("own", 0, 2), ("own", 2, 2), ("own", 4, 3)),
 )
+ACROSS = ((5, 6, 7), ())
 INNER = (
     ("xm", 1, 0),
+    ("xy", 1, 0),
     ("xf", 1, 0),
+    ("wp", 1, 2),
+    ("wp", 4, 1),
+    ("ox", 7, 0),
+    ("ox", 1, 0),
+    ("wp", 7, 1),
+    ("ko", 4, 0),
+    ("wd", 1, 0),
+    ("wp", 1, 1),
+    ("ox", 4, 0),
+    ("wp", 0, 2),
+    ("ox", 5, 0),
+    ("bias", 0, 0),
+    ("rx", 2, 1),
+    ("wd", 0, 0),
+    ("ox", 3, 0),
+    ("ox", 6, 0),
+    ("wp", 0, 1),
+    ("wp", 3, 1),
     ("xf", 0, 0),
-    ("xy", 1, 0),
-    ("wp", 0, 2),
-    ("wp", 1, 1),
+    ("xm", 0, 0),
+    ("ko", 1, 0),
+    ("rd", 1, 0),
+    ("rx", 2, 0),
+    ("rd", 4, 0),
+    ("kw", 0, 1),
+    ("rw", 4, 2),
+    ("rc", 1, 0),
+    ("ko", 3, 0),
+    ("rx", 3, 1),
+    ("ox", 2, 0),
+    ("xy", 0, 0),
+    ("ry", 1, 1),
+    ("wd", 3, 0),
+    ("rw", 4, 1),
+    ("ry", 2, 1),
+    ("rc", 2, 0),
+    ("rw", 4, 3),
+    ("kw", 1, 1),
+    ("rx", 3, 0),
+    ("rw", 7, 1),
+    ("rc", 4, 2),
+    ("rw", 1, 3),
+    ("ko", 2, 0),
+    ("rc", 3, 0),
+    ("rc", 4, 0),
+    ("wd", 2, 0),
+    ("rw", 1, 2),
+    ("ry", 1, 0),
+    ("kw", 4, 2),
+    ("kw", 4, 1),
+    ("wp", 2, 1),
+    ("rw", 0, 1),
+    ("rc", 4, 3),
+    ("kw", 4, 3),
+    ("rc", 4, 1),
+    ("kw", 1, 2),
+    ("wp", 6, 1),
+    ("rw", 3, 2),
+    ("pm", 1, 4),
+    ("ko", 0, 0),
+    ("rw", 1, 1),
+    ("wp", 3, 2),
+    ("pm", 0, 4),
+    ("rd", 3, 0),
+    ("rw", 3, 1),
+    ("wd", 4, 0),
+    ("ko", 7, 0),
+    ("rd", 2, 0),
+    ("wp", 4, 2),
+    ("wp", 5, 1),
+    ("kw", 2, 2),
+    ("kw", 1, 3),
+    ("rw", 2, 1),
+    ("rc", 1, 2),
+    ("kw", 3, 2),
+    ("rc", 3, 2),
+    ("kw", 2, 1),
+    ("rc", 1, 3),
+    ("rw", 2, 2),
+    ("rc", 1, 1),
+    ("pm", 2, 4),
+    ("rw", 3, 3),
+    ("pm", 2, 1),
+    ("rc", 7, 0),
+    ("rd", 0, 0),
+    ("rw", 2, 3),
+    ("wp", 2, 2),
+    ("rc", 3, 1),
+    ("kw", 3, 1),
     ("ox", 0, 0),
-    ("ox", 1, 0),
-    ("ko", 0, 0),
-    ("ox", 6, 0),
-    ("ko", 1, 0),
-    ("wp", 3, 1),
-    ("bias", 0, 0),
+    ("ry", 3, 1),
+    ("kw", 0, 3),
+    ("pm", 0, 1),
+    ("ko", 5, 0),
+    ("rw", 0, 2),
+    ("rw", 0, 3),
+    ("kw", 5, 1),
+    ("pm", 1, 1),
+    ("rc", 6, 0),
+    ("kw", 3, 3),
+    ("rw", 6, 1),
+    ("rc", 3, 3),
+    ("rc", 2, 1),
+    ("kw", 0, 2),
+    ("ry", 2, 0),
+    ("rc", 0, 1),
+    ("rc", 2, 2),
+    ("kw", 2, 3),
+    ("rc", 2, 3),
+    ("pm", 1, 3),
     ("rc", 0, 0),
-    ("ox", 3, 0),
     ("ko", 6, 0),
-    ("rx", 2, 1),
-    ("wp", 2, 1),
-    ("rc", 1, 0),
-    ("ox", 2, 0),
-    ("ko", 3, 0),
-    ("rc", 6, 0),
-    ("ko", 2, 0),
-    ("rx", 2, 0),
-    ("ry", 2, 0),
-    ("rw", 3, 1),
-    ("wd", 1, 0),
-    ("rc", 3, 0),
-    ("ox", 4, 0),
-    ("kw", 3, 1),
-    ("rd", 1, 0),
-    ("wd", 0, 0),
-    ("rc", 2, 0),
-    ("rw", 1, 1),
-    ("ko", 4, 0),
-    ("rd", 3, 0),
-    ("rc", 3, 1),
-    ("rw", 3, 2),
-    ("kw", 1, 1),
-    ("wp", 1, 2),
-    ("rc", 4, 0),
-    ("kw", 3, 2),
+    ("pm", 1, 2),
+    ("pm", 2, 2),
+    ("rw", 6, 3),
+    ("rc", 0, 2),
     ("ry", 3, 0),
-    ("xm", 0, 0),
-    ("wp", 6, 1),
-    ("rw", 0, 2),
-    ("rc", 1, 1),
-    ("kw", 0, 2),
-    ("rw", 1, 2),
-    ("rx", 3, 0),
-    ("rc", 3, 2),
-    ("rw", 3, 3),
-    ("kw", 1, 2),
-    ("wp", 0, 1),
-    ("rc", 0, 2),
-    ("rw", 1, 3),
-    ("kw", 3, 3),
-    ("wp", 4, 1),
-    ("rc", 1, 2),
-    ("ox", 5, 0),
-    ("kw", 1, 3),
-    ("rx", 3, 1),
-    ("ry", 2, 1),
-    ("rc", 3, 3),
-    ("ko", 5, 0),
-    ("ry", 1, 1),
+    ("rw", 5, 1),
     ("pm", 0, 3),
-    ("wp", 4, 2),
-    ("rc", 1, 3),
-    ("rw", 4, 1),
-    ("kw", 4, 1),
-    ("pm", 0, 1),
-    ("rw", 2, 2),
-    ("rc", 5, 0),
-    ("rw", 2, 1),
-    ("kw", 2, 2),
-    ("wp", 3, 2),
-    ("rc", 4, 1),
-    ("rd", 5, 0),
-    ("rw", 0, 1),
-    ("kw", 2, 1),
-    ("rc", 2, 2),
-    ("rd", 2, 0),
-    ("rw", 6, 1),
-    ("kw", 0, 1),
-    ("wp", 2, 2),
-    ("rd", 0, 0),
-    ("rc", 2, 1),
+    ("kw", 6, 3),
+    ("rw", 6, 2),
     ("kw", 6, 1),
-    ("rw", 5, 3),
-    ("wd", 3, 0),
-    ("wp", 5, 1),
-    ("rc", 0, 1),
-    ("kw", 5, 3),
-    ("wd", 2, 0),
-    ("rw", 2, 3),
-    ("ry", 3, 1),
-    ("rc", 6, 1),
-    ("wd", 4, 0),
-    ("kw", 2, 3),
-    ("rw", 0, 3),
-    ("xy", 0, 0),
-    ("rc", 5, 3),
-    ("kw", 0, 3),
-    ("rw", 5, 1),
-    ("rc", 2, 3),
-    ("kw", 5, 1),
-    ("ry", 1, 0),
-    ("pm", 0, 2),
     ("rc", 0, 3),
     ("pm", 0, 0),
+    ("rc", 6, 3),
+    ("pm", 2, 0),
+    ("rw", 7, 3),
+    ("pm", 0, 2),
+    ("rc", 5, 0),
+    ("pm", 3, 1),
+    ("rc", 6, 1),
+    ("kw", 7, 3),
     ("rc", 5, 1),
-    ("rw", 4, 2),
-    ("kw", 4, 2),
+    ("rw", 7, 2),
+    ("pm", 1, 0),
+    ("pm", 3, 2),
+    ("kw", 6, 2),
+    ("pm", 2, 3),
+    ("rc", 6, 2),
     ("rw", 5, 2),
+    ("kw", 7, 2),
+    ("pm", 3, 3),
+    ("om", 1, 6),
+    ("om", 0, 6),
+    ("pm", 3, 0),
+    ("kw", 7, 1),
+    ("rw", 5, 3),
+    ("pm", 3, 4),
+    ("rc", 7, 1),
+    ("rc", 7, 2),
+    ("rc", 7, 3),
+    ("om", 0, 7),
+    ("fin", 0, 6),
+    ("rc", 5, 2),
+    ("kw", 5, 3),
     ("kw", 5, 2),
-    ("pm", 1, 0),
-    ("rc", 4, 2),
-    ("pm", 1, 1),
-    ("rd", 4, 0),
-    ("pm", 1, 2),
-    ("rw", 6, 2),
-    ("kw", 6, 2),
-    ("pm", 1, 3),
-    ("rc", 5, 2),
-    ("rw", 4, 3),
-    ("rd", 6, 0),
-    ("kw", 4, 3),
+    ("fin", 2, 6),
+    ("rc", 5, 3),
+    ("fin", 1, 7),
+    ("om", 1, 7),
+    ("om", 1, 5),
+    ("fin", 3, 6),
     ("om", 0, 5),
-    ("rc", 6, 2),
-    ("om", 1, 5),
-    ("rw", 6, 3),
-    ("rc", 4, 3),
-    ("kw", 6, 3),
+    ("fin", 2, 5),
+    ("fin", 3, 5),
+    ("fin", 1, 6),
     ("fin", 0, 5),
     ("fin", 1, 5),
-    ("om", 0, 4),
-    ("om", 1, 4),
-    ("fin", 0, 4),
-    ("fin", 1, 4),
-    ("rc", 6, 3),
-    ("om", 0, 6),
-    ("om", 1, 6),
-    ("fin", 0, 6),
-    ("fin", 1, 6),
+    ("fin", 0, 7),
+    ("fin", 3, 7),
+    ("fin", 2, 7),
 )
 OUTER = (
+    ("xy", 1, 0),
+    ("xm", 1, 0),
+    ("wp", 4, 2),
+    ("wd", 4, 0),
+    ("xy", 0, 0),
+    ("wd", 1, 0),
+    ("wp", 1, 1),
+    ("bias", 0, 0),
+    ("rw", 1, 2),
+    ("wp", 3, 1),
+    ("ko", 1, 0),
+    ("ox", 1, 0),
+    ("xf", 1, 0),
+    ("ox", 0, 0),
+    ("wp", 0, 1),
+    ("rw", 1, 1),
+    ("rd", 1, 0),
+    ("xf", 0, 0),
+    ("rc", 0, 0),
+    ("ry", 1, 1),
+    ("kw", 1, 3),
     ("xm", 0, 0),
-    ("xy", 1, 0),
+    ("rw", 0, 1),
+    ("rw", 1, 3),
+    ("ox", 4, 0),
+    ("wp", 1, 2),
+    ("rc", 1, 2),
+    ("kw", 1, 2),
+    ("rd", 0, 0),
+    ("ry", 1, 0),
+    ("ko", 0, 0),
+    ("rc", 0, 1),
+    ("rc", 1, 0),
+    ("rc", 1, 3),
     ("wp", 3, 2),
-    ("wp", 0, 1),
+    ("ko", 4, 0),
+    ("rc", 1, 1),
+    ("rw", 0, 3),
+    ("kw", 1, 1),
+    ("ry", 2, 0),
+    ("rw", 0, 2),
+    ("kw", 0, 3),
+    ("pm", 0, 1),
+    ("ry", 2, 1),
+    ("pm", 2, 1),
+    ("wd", 3, 0),
+    ("ox", 3, 0),
+    ("rc", 0, 2),
+    ("rw", 3, 1),
+    ("ko", 3, 0),
+    ("wp", 2, 2),
+    ("ry", 3, 1),
+    ("kw", 0, 1),
+    ("wd", 2, 0),
+    ("ry", 3, 0),
+    ("rd", 3, 0),
+    ("pm", 1, 1),
+    ("we", 6, 0),
+    ("kw", 0, 2),
+    ("rc", 0, 3),
+    ("pm", 0, 0),
+    ("pm", 1, 0),
+    ("kw", 3, 2),
+    ("wd", 0, 0),
+    ("wp", 0, 2),
+    ("we", 7, 0),
+    ("pm", 3, 0),
+    ("rw", 3, 2),
+    ("kw", 3, 3),
+    ("pm", 3, 1),
+    ("ko", 2, 0),
     ("ox", 2, 0),
-    ("ox", 0, 0),
-    ("ko", 2, 0),
-    ("ox", 3, 0),
-    ("ko", 0, 0),
-    ("wd", 3, 0),
-    ("bias", 0, 0),
-    ("rc", 2, 0),
-    ("ox", 4, 0),
-    ("ko", 3, 0),
-    ("ry", 1, 1),
-    ("wd", 0, 0),
-    ("wp", 1, 1),
-    ("rc", 0, 0),
-    ("ko", 4, 0),
-    ("rw", 0, 2),
-    ("wd", 1, 0),
+    ("re", 6, 0),
+    ("rw", 3, 3),
     ("rc", 3, 0),
-    ("xf", 0, 0),
-    ("rw", 0, 1),
-    ("kw", 0, 2),
-    ("ry", 2, 1),
-    ("wp", 0, 2),
-    ("rc", 4, 0),
-    ("ox", 1, 0),
-    ("rc", 0, 2),
-    ("ko", 1, 0),
-    ("rw", 1, 1),
-    ("ry", 2, 0),
-    ("wp", 1, 2),
-    ("rc", 0, 1),
-    ("kw", 0, 1),
-    ("kw", 1, 1),
-    ("xf", 1, 0),
-    ("rd", 1, 0),
-    ("rc", 1, 0),
-    ("xm", 1, 0),
-    ("rd", 0, 0),
-    ("rc", 1, 1),
-    ("rw", 1, 2),
-    ("kw", 1, 2),
-    ("wp", 2, 2),
-    ("xy", 0, 0),
-    ("rw", 1, 3),
-    ("kw", 1, 3),
-    ("ry", 1, 0),
-    ("rw", 0, 3),
-    ("wd", 5, 0),
-    ("rc", 1, 2),
-    ("kw", 0, 3),
-    ("wd", 2, 0),
-    ("rc", 1, 3),
-    ("ry", 3, 0),
-    ("rc", 0, 3),
-    ("ry", 3, 1),
-    ("pm", 0, 0),
-    ("pm", 0, 1),
     ("wp", 2, 1),
+    ("wp", 6, 2),
     ("rw", 4, 2),
-    ("kw", 4, 2),
     ("wp", 4, 1),
-    ("pm", 1, 0),
-    ("wp", 3, 1),
-    ("rw", 3, 2),
-    ("pm", 1, 1),
-    ("kw", 3, 2),
-    ("rw", 2, 1),
-    ("rc", 4, 2),
-    ("rw", 2, 2),
-    ("kw", 2, 1),
-    ("rd", 3, 0),
-    ("rc", 3, 2),
-    ("kw", 2, 2),
-    ("rw", 4, 1),
-    ("wp", 4, 2),
-    ("rd", 2, 0),
-    ("rc", 2, 1),
-    ("kw", 4, 1),
-    ("rw", 3, 1),
-    ("rc", 2, 2),
+    ("re", 7, 0),
+    ("rc", 3, 3),
+    ("rc", 3, 1),
     ("rd", 4, 0),
     ("kw", 3, 1),
+    ("rw", 2, 1),
+    ("kw", 2, 1),
+    ("rc", 3, 2),
+    ("om", 0, 3),
+    ("rw", 4, 1),
+    ("wp", 7, 2),
+    ("om", 1, 3),
+    ("rw", 2, 2),
     ("wp", 5, 2),
+    ("rc", 2, 0),
+    ("rc", 4, 0),
+    ("we", 5, 0),
+    ("kw", 4, 1),
+    ("re", 5, 0),
+    ("rw", 4, 3),
+    ("kw", 4, 2),
+    ("rd", 2, 0),
+    ("rc", 4, 1),
+    ("kw", 4, 3),
+    ("kw", 2, 3),
     ("rw", 2, 3),
-    ("rc", 4, 1),
-    ("rw", 3, 3),
-    ("kw", 2, 3),
-    ("wd", 4, 0),
-    ("rc", 3, 1),
-    ("kw", 3, 3),
-    ("rw", 4, 3),
-    ("wp", 6, 2),
+    ("kw", 2, 2),
+    ("rc", 4, 2),
+    ("rc", 4, 3),
+    ("rc", 2, 2),
+    ("pm", 2, 0),
+    ("rc", 2, 1),
+    ("fin", 0, 3),
+    ("om", 0, 4),
+    ("fin", 1, 3),
+    ("om", 1, 4),
     ("rc", 2, 3),
-    ("kw", 4, 3),
+    ("fin", 1, 4),
     ("om", 0, 2),
-    ("wd", 6, 0),
-    ("rc", 3, 3),
     ("om", 1, 2),
-    ("om", 0, 3),
-    ("om", 1, 3),
-    ("rc", 4, 3),
-    ("fin", 0, 3),
+    ("fin", 1, 2),
+    ("fin", 3, 4),
+    ("fin", 2, 2),
+    ("fin", 0, 4),
+    ("fin", 3, 2),
+    ("fin", 3, 3),
+    ("fin", 2, 3),
+    ("fin", 2, 4),
     ("fin", 0, 2),
-    ("om", 0, 4),
-    ("om", 1, 4),
-    ("fin", 0, 4),
-    ("fin", 1, 2),
-    ("fin", 1, 4),
-    ("fin", 1, 3),
 )
 
 
@@ -349,6 +394,11 @@
     return result[None]
 
 
+def incoming(kind):
+    chunks = [c for c in CHUNKS[1 - kind] if c[0] == "far"]
+    return [c[1:] for c in chunks + [c for c in CHUNKS[kind] if c[0] == "extra"]]
+
+
 def chunk_of(kind, j):
     what, first, count = CHUNKS[kind][j]
     return what, first, count, sum(c[2] for c in CHUNKS[kind][:j])
@@ -368,6 +418,7 @@
     wsend,
     wbuf,
     dbuf,
+    ebuf,
     psend,
     pbuf,
     acc,
@@ -381,6 +432,7 @@
     wx_recv,
     wc_recv,
     d_recv,
+    e_recv,
     w_send,
     p_recv,
     p_send,
@@ -445,19 +497,19 @@
     def own_x(which, device, side, piece):
         return remote(
             piece_of(xsend.at[which], piece),
-            piece_of(xbuf.at[side, z], piece),
+            piece_of(xbuf.at[side, half, lax.rem(z, 2)], piece),
             x_send.at[0],
-            x1_recv if side else x_recv.at[z, piece],
+            x1_recv.at[half] if side else x_recv.at[z, piece],
             (inst, device),
         )
 
     def relay_x(way, block, piece):
         device, side = ((z_mate * 2 + y, 0), (z * 2 + 1 - y, 1))[way]
         return remote(
-            piece_of(xbuf.at[0, block], piece),
-            piece_of(xbuf.at[side, block], piece),
+            piece_of(xbuf.at[0, block // 2, lax.rem(block, 2)], piece),
+            piece_of(xbuf.at[side, block // 2, lax.rem(block, 2)], piece),
             x_send.at[1 + way],
-            x1_recv if side else x_recv.at[block, piece],
+            x1_recv.at[block // 2] if side else x_recv.at[block, piece],
             (inst, device),
         )
 
@@ -573,7 +625,7 @@
 
     each(inner, lambda: early(INNER))
     each(jnp.logical_not(inner), lambda: early(OUTER))
-    xbuf[0, z] = xsend[half]
+    xbuf[0, half, lax.rem(z, 2)] = xsend[half]
 
     weight_load.wait()
     for rank in range(TP):
@@ -587,9 +639,8 @@
                 part = w_ref[:, source + inside : source + inside + LANES].astype(jnp.bfloat16).astype(jnp.float32)
                 wsend[rank, (target + inside) // LANES] = (part * gain).astype(jnp.bfloat16)
 
-    def product(kind, m, j):
+    def product(kind, lhs, j):
         _, first, count, at = chunk_of(kind, j)
-        lhs = xbuf[m].reshape(4 * tokens, 4 * half_block)
         result = []
         for t in range(0, count, 2):
             width = min(2, count - t)
@@ -626,7 +677,7 @@
                 once(
                     ("x", block, piece),
                     lambda piece=piece: arrived(
-                        piece_of(xbuf.at[0, places[block]], piece), x_recv.at[places[block], piece]
+                        mine(block, piece), x_recv.at[places[block], piece]
                     ),
                 )
 
@@ -642,25 +693,30 @@
 
             once(("c", j), action)
 
-        def need_tokens(m):
-            for block in (1, 2, 3):
-                need_x(block)
-            if m:
-                once("x1", lambda: arrived(xbuf.at[1], x1_recv))
+        def mine(block, piece):
+            return piece_of(xbuf.at[0, places[block] // 2, lax.rem(places[block], 2)], piece)
+
+        def need_tokens(unit):
+            if unit < 2:
+                for block in ((1,), (2, 3))[unit]:
+                    need_x(block)
+            else:
+                part = half if unit == 2 else 1 - half
+                once(("y", unit), lambda: arrived(xbuf.at[1, part], x1_recv.at[part]))
 
         places = (z, z_mate, z_near, z_end)
 
         def step_rx(block, piece):
             once(
                 ("x", block, piece),
-                lambda: arrived(piece_of(xbuf.at[0, places[block]], piece), x_recv.at[places[block], piece]),
+                lambda: arrived(mine(block, piece), x_recv.at[places[block], piece]),
             )
             relay_x(0, places[block], piece).start()
 
         def step_ry(block, piece):
             once(
                 ("x", block, piece),
-                lambda: arrived(piece_of(xbuf.at[0, places[block]], piece), x_recv.at[places[block], piece]),
+                lambda: arrived(mine(block, piece), x_recv.at[places[block], piece]),
             )
             relay_x(1, places[block], piece).start()
 
@@ -679,6 +735,19 @@
                 fresh(other, z_mate, j, 1 - y), target, w_send.at[2], d_recv.at[j], (inst, z_mate * 2 + y)
             ).start()
 
+        def step_we(j, _):
+            _, _, count, at = chunk_of(other, j)
+            remote(
+                fresh(other, z_mate, j, 1 - y), ebuf.at[pl.ds(at, count)], w_send.at[6], e_recv.at[j], (inst, z * 2 + 1 - y)
+            ).start()
+
+        def step_re(j, _):
+            _, _, count, at = chunk_of(other, j)
+            source = ebuf.at[pl.ds(at, count)]
+            arrived(source, e_recv.at[j])
+            target = held(other, slot_of(inst, 1), j)
+            remote(source, target, w_send.at[7], w_recv.at[2, j], (inst, z_mate * 2 + y)).start()
+
         def step_rd(j, _):
             _, _, count, at = chunk_of(kind, j)
             source = dbuf.at[pl.ds(at, count)]
@@ -712,39 +781,52 @@
             arrived(block, wx_recv.at[k, j])
             remote(block, block, w_send.at[5], wc_recv.at[j], (core_peer, me)).start()
 
-        def step_pm(m, j):
-            need_tokens(m)
+        def step_pm(unit, j):
+            need_tokens(unit)
             need_chunk(j)
             what, first, count, at = chunk_of(kind, j)
-            for t, value in product(kind, m, j):
-                psend[m, at + t] = value.astype(jnp.bfloat16)
+            side, part = unit // 2, (1 - half if unit % 2 else half)
+            lhs = xbuf[side, part].reshape(2 * tokens, 4 * half_block)
+            for t, value in product(kind, lhs, j):
+                psend[side, part, at + t] = value.astype(jnp.bfloat16)
             target = other if what == "far" else kind
-            index = [c[:3] for c in CHUNKS[target]].index(("own", first, count))
+            index = incoming(target).index((first, count))
             remote(
-                psend.at[m, pl.ds(at, count)],
-                pbuf.at[m, pl.ds(first, count)],
+                psend.at[side, part, pl.ds(at, count)],
+                pbuf.at[side, part, pl.ds(first, count)],
                 p_send.at[0],
-                p_recv.at[m, index],
+                p_recv.at[side, part, index],
                 (inst, (z_pair if what == "far" else z_near) * 2 + y),
             ).start()
 
         def step_om(m, j):
-            need_tokens(m)
+            for unit in (0, 1) if m == 0 else (2, 3):
+                need_tokens(unit)
             need_chunk(j)
             first = chunk_of(kind, j)[1]
-            for t, value in product(kind, m, j):
-                acc[m, first + t] = value
-
-        def step_fin(m, j):
+            lhs = xbuf[m].reshape(4 * tokens, 4 * half_block)
+            for t, value in product(kind, lhs, j):
+                for part in range(2):
+                    acc[m, part, first + t] = value[part * 2 * tokens : (part + 1) * 2 * tokens]
+
+        def step_fin(unit, j):
             once("bias", finish_bias)
             _, first, count, _ = chunk_of(kind, j)
-            arrived(pbuf.at[m, pl.ds(first, count)], p_recv.at[m, j])
-            where = 1 - y if m else y
+            side, part = unit // 2, (1 - half if unit % 2 else half)
+            for index, (low, extent) in enumerate(incoming(kind)):
+                if low < first + count and first < low + extent:
+                    once(
+                        ("p", unit, index),
+                        lambda: arrived(
+                            pbuf.at[side, part, pl.ds(low, extent)], p_recv.at[side, part, index]
+                        ),
+                    )
+            where = 1 - y if side else y
             for t in range(first, first + count):
-                value = acc[m, t] + pbuf[m, t].astype(jnp.float32) + bias_row(column_of(t) // group)
+                value = acc[side, part, t] + pbuf[side, part, t].astype(jnp.float32) + bias_row(column_of(t) // group)
                 value = value.astype(jnp.bfloat16)
-                for k in range(4):
-                    out_ref[k, where, :, t * LANES : (t + 1) * LANES] = value[k * tokens : (k + 1) * tokens]
+                for k in range(2):
+                    out_ref[part * 2 + k, where, :, t * LANES : (t + 1) * LANES] = value[k * tokens : (k + 1) * tokens]
 
         def step_bias(*_):
             send_bias(False)
@@ -758,6 +840,8 @@
             wp=step_wp,
             wd=step_wd,
             rd=step_rd,
+            we=step_we,
+            re=step_re,
             ox=step_ox,
             ko=step_ko,
             rw=step_rw,
@@ -774,15 +858,25 @@
 
         counts = [sum(c[2] for c in CHUNKS[way]) for way in range(2)]
         sent = counts[kind] - tiles
-        once("sent_x", lambda: arrived(xbuf.at[0, pl.ds(0, 3)], x_send.at[0]))
-        once("sent_y", lambda: arrived(xbuf.at[0, pl.ds(0, 3)], x_send.at[2]))
+        three = xbuf.at[0, :, :, pl.ds(0, 3 * tokens // 4)]
+        arrived(three, x_send.at[0])
+        arrived(three, x_send.at[2])
         if kind == 0:
-            arrived(xbuf.at[0, pl.ds(0, 2)], x_send.at[1])
-        for way, target in enumerate((kind, other, other, kind)):
-            arrived(wbuf.at[0, pl.ds(0, counts[target])], w_send.at[way])
+            arrived(xbuf.at[0, 0], x_send.at[1])
+        across = [sum(c[2] for j, c in enumerate(CHUNKS[way]) if j in ACROSS[way]) for way in range(2)]
+        for way, extent in (
+            (0, counts[kind]),
+            (1, counts[other]),
+            (2, counts[other] - across[other]),
+            (3, counts[kind] - across[kind]),
+            (6, across[other]),
+            (7, across[other]),
+        ):
+            if extent:
+                arrived(wbuf.at[0, pl.ds(0, extent)], w_send.at[way])
         arrived(wbuf.at[pl.ds(0, 4), pl.ds(0, counts[kind])], w_send.at[4])
         arrived(wbuf.at[pl.ds(0, 8), pl.ds(0, counts[kind])], w_send.at[5])
-        arrived(psend.at[:, pl.ds(0, sent)], p_send.at[0])
+        arrived(psend.at[:, :, pl.ds(0, sent)], p_send.at[0])
 
     each(inner, lambda: run(0, INNER))
     each(jnp.logical_not(inner), lambda: run(1, OUTER))
@@ -803,38 +897,40 @@
     low, wide = jnp.bfloat16, jnp.float32
     result = pl.pallas_call(
         functools.partial(kernel, dims),
-        out_shape=jax.ShapeDtypeStruct((4, 2, count, tiles * LANES), low),
+        out_shape=pltpu.VMEM((4, 2, count, tiles * LANES), low),
         in_specs=[anywhere, vmem, anywhere, vmem],
         out_specs=vmem,
         scratch_shapes=[
             pltpu.VMEM((count, depth), low),
             pltpu.VMEM((rows, master_qkv.shape[1]), wide),
             pltpu.VMEM((2, count, depth // 2), low),
-            pltpu.VMEM((2, 4, count, depth // 2), low),
+            pltpu.VMEM((2, 2, 2, count, depth // 2), low),
             pltpu.VMEM((TP, tiles, rows, LANES), low),
             pltpu.VMEM((4 * inst_count, held, rows, LANES), low),
             pltpu.VMEM((held, rows, LANES), low),
-            pltpu.VMEM((2, held - tiles, 4 * count, LANES), low),
-            pltpu.VMEM((2, tiles, 4 * count, LANES), low),
-            pltpu.VMEM((2, tiles, 4 * count, LANES), wide),
+            pltpu.VMEM((held, rows, LANES), low),
+            pltpu.VMEM((2, 2, held - tiles, 2 * count, LANES), low),
+            pltpu.VMEM((2, 2, tiles, 2 * count, LANES), low),
+            pltpu.VMEM((2, 2, tiles, 2 * count, LANES), wide),
             pltpu.VMEM((8, LANES), wide),
             pltpu.VMEM((devices, 8, LANES), wide),
             dma((2,)),
             dma((4, pieces)),
-            dma,
+            dma((2,)),
             dma((3,)),
             dma((3, most)),
             dma((4, most)),
             dma((most,)),
             dma((most,)),
-            dma((6,)),
-            dma((2, most)),
+            dma((most,)),
+            dma((8,)),
+            dma((2, 2, most)),
             dma((1,)),
             dma((devices,)),
             dma((devices,)),
         ],
         compiler_params=pltpu.CompilerParams(
-            collective_id=0, has_side_effects=True, vmem_limit_bytes=60 * 1024 * 1024
+            collective_id=0, has_side_effects=True, vmem_limit_bytes=56 * 1024 * 1024
         ),
     )(tokens, norm_gain.reshape(1, rows), master_qkv, qkv_bias.reshape(1, -1))
     return result.reshape(1, shard_count * count, tiles * LANES)

time: 80.5 us -> 76.7 us (0.953)
  Pallas kernels: 77.8 us -> 75.6 us
  local copies, waits for them, and re-layouts: 2.18 us -> 0.93 us
    pallas_call x1, Pallas kernels: 77.8 us -> 75.6 us  [kernel_device(): pl.pallas_call(functools.partial(kernel, dims), out_shape=pltpu.VMEM((4,...]
    unnamed x1, local copies, waits for them, and re-layouts: 2.18 us -> 0.93 us
where the time goes in v4:
time: 76.7 us; the launch traced here: 76.5 us
  Pallas kernels  75.6 us (99%)
  local copies, waits for them, and re-layouts  0.93 us (1%)
    pallas_call x1, Pallas kernels, kernel_device(): pl.pallas_call(functools.partial(kernel, dims), out_shape=pltpu.VMEM((4,...  75.6 us

profile of v4, /device:TPU:0, one launch (start us, length us, event | category | flops | bytes accessed | tf_op | source)
XLA Modules:
  0.0 76.5 jit_solution(7086864241150710879)
XLA Ops:
  0.0 75.6 %shard_map.46 = bf16[4,2,64,896]{3,2,1,0:T(8,128)(2,1)S(1)} custom-call(bf16[64,5120]{1,0:T(8,128)(2,1)} %tok_hbm.1, f32[1,160]{1,0:T(1,128)} %bitcast.4, f32[160,7168]{1,0:T(8,128)} %w_hbm.1, f32[1,224]{1,0:T(1,128)} %bitcast.5), custom_call_target="tpu_custom_call" | custom-call | tf_op jit(solution)/shard_map/pallas_call | solution.py:898
  75.6 0.9 %copy.6 = bf16[1,512,896]{2,1,0:T(8,128)(2,1)} copy(bf16[1,512,896]{2,1,0:T(8,128)(2,1)S(1)} %bitcast.3) | data formatting | bytes 1835008

commit v5 on v4

--- a/solution.py
+++ b/solution.py
@@ -24,309 +24,313 @@
 ACROSS = ((5, 6, 7), ())
 INNER = (
     ("xm", 1, 0),
-    ("xy", 1, 0),
     ("xf", 1, 0),
-    ("wp", 1, 2),
+    ("xf", 0, 0),
+    ("xy", 0, 0),
+    ("wp", 0, 2),
     ("wp", 4, 1),
-    ("ox", 7, 0),
+    ("ox", 5, 0),
+    ("ox", 2, 0),
+    ("ko", 5, 0),
+    ("ox", 0, 0),
+    ("ko", 2, 0),
+    ("xm", 0, 0),
+    ("rc", 5, 0),
     ("ox", 1, 0),
-    ("wp", 7, 1),
-    ("ko", 4, 0),
-    ("wd", 1, 0),
-    ("wp", 1, 1),
+    ("ko", 0, 0),
     ("ox", 4, 0),
-    ("wp", 0, 2),
-    ("ox", 5, 0),
-    ("bias", 0, 0),
-    ("rx", 2, 1),
-    ("wd", 0, 0),
-    ("ox", 3, 0),
-    ("ox", 6, 0),
-    ("wp", 0, 1),
-    ("wp", 3, 1),
-    ("xf", 0, 0),
-    ("xm", 0, 0),
     ("ko", 1, 0),
-    ("rd", 1, 0),
-    ("rx", 2, 0),
-    ("rd", 4, 0),
-    ("kw", 0, 1),
-    ("rw", 4, 2),
-    ("rc", 1, 0),
-    ("ko", 3, 0),
-    ("rx", 3, 1),
-    ("ox", 2, 0),
-    ("xy", 0, 0),
-    ("ry", 1, 1),
-    ("wd", 3, 0),
-    ("rw", 4, 1),
     ("ry", 2, 1),
     ("rc", 2, 0),
+    ("wp", 1, 1),
+    ("rc", 0, 0),
+    ("ko", 4, 0),
+    ("rw", 4, 1),
+    ("rc", 1, 0),
+    ("rx", 2, 0),
+    ("wd", 1, 0),
+    ("kw", 4, 1),
+    ("rw", 1, 2),
+    ("rd", 4, 0),
+    ("rc", 4, 0),
+    ("ry", 2, 0),
+    ("kw", 1, 2),
+    ("rw", 4, 2),
+    ("wp", 3, 2),
+    ("rc", 4, 1),
+    ("kw", 4, 2),
+    ("wd", 0, 0),
+    ("rc", 1, 2),
     ("rw", 4, 3),
+    ("rx", 2, 1),
+    ("rw", 1, 1),
+    ("kw", 4, 3),
+    ("ry", 3, 1),
+    ("rc", 4, 2),
+    ("ox", 3, 0),
     ("kw", 1, 1),
     ("rx", 3, 0),
+    ("ry", 3, 0),
+    ("rc", 4, 3),
+    ("ox", 6, 0),
+    ("ko", 3, 0),
+    ("wp", 1, 2),
+    ("wp", 6, 1),
+    ("pm", 1, 4),
+    ("rc", 1, 1),
+    ("ox", 7, 0),
+    ("pm", 0, 4),
+    ("rc", 3, 0),
+    ("ko", 6, 0),
+    ("ko", 7, 0),
+    ("rw", 2, 2),
+    ("rx", 3, 1),
+    ("rc", 6, 0),
+    ("rd", 2, 0),
+    ("pm", 3, 4),
+    ("wd", 4, 0),
+    ("wp", 3, 1),
+    ("kw", 2, 2),
+    ("rw", 6, 1),
+    ("wp", 5, 1),
+    ("rc", 7, 0),
+    ("kw", 6, 1),
+    ("wd", 3, 0),
+    ("rc", 2, 2),
+    ("rw", 3, 2),
+    ("kw", 3, 2),
+    ("rd", 1, 0),
+    ("rw", 3, 1),
+    ("wp", 0, 1),
+    ("rc", 6, 1),
+    ("kw", 3, 1),
+    ("wp", 4, 2),
+    ("rw", 5, 1),
+    ("rd", 3, 0),
+    ("rc", 3, 2),
+    ("wp", 2, 2),
+    ("wp", 2, 1),
+    ("rw", 1, 3),
+    ("rc", 3, 1),
+    ("kw", 1, 3),
+    ("rw", 0, 1),
+    ("wp", 7, 1),
+    ("wd", 2, 0),
+    ("rc", 5, 1),
+    ("rw", 2, 3),
+    ("kw", 0, 1),
+    ("ry", 1, 1),
+    ("kw", 2, 3),
+    ("rc", 1, 3),
+    ("rw", 2, 1),
+    ("pw", 1, 0),
+    ("bias", 0, 0),
+    ("rc", 0, 1),
+    ("rw", 3, 3),
+    ("kw", 2, 1),
+    ("pm", 0, 1),
+    ("pm", 1, 1),
+    ("pm", 3, 1),
+    ("rc", 2, 3),
+    ("kw", 3, 3),
     ("rw", 7, 1),
-    ("rc", 4, 2),
-    ("rw", 1, 3),
-    ("ko", 2, 0),
-    ("rc", 3, 0),
-    ("rc", 4, 0),
-    ("wd", 2, 0),
-    ("rw", 1, 2),
+    ("rc", 2, 1),
+    ("kw", 5, 1),
+    ("kw", 7, 1),
+    ("rd", 0, 0),
+    ("xy", 1, 0),
+    ("rw", 0, 2),
     ("ry", 1, 0),
-    ("kw", 4, 2),
-    ("kw", 4, 1),
-    ("wp", 2, 1),
-    ("rw", 0, 1),
-    ("rc", 4, 3),
-    ("kw", 4, 3),
-    ("rc", 4, 1),
-    ("kw", 1, 2),
-    ("wp", 6, 1),
-    ("rw", 3, 2),
-    ("pm", 1, 4),
-    ("ko", 0, 0),
-    ("rw", 1, 1),
-    ("wp", 3, 2),
-    ("pm", 0, 4),
-    ("rd", 3, 0),
-    ("rw", 3, 1),
-    ("wd", 4, 0),
-    ("ko", 7, 0),
-    ("rd", 2, 0),
-    ("wp", 4, 2),
-    ("wp", 5, 1),
-    ("kw", 2, 2),
-    ("kw", 1, 3),
-    ("rw", 2, 1),
-    ("rc", 1, 2),
-    ("kw", 3, 2),
-    ("rc", 3, 2),
-    ("kw", 2, 1),
-    ("rc", 1, 3),
-    ("rw", 2, 2),
-    ("rc", 1, 1),
+    ("pm", 0, 2),
+    ("pm", 1, 2),
+    ("rc", 3, 3),
+    ("pm", 3, 2),
+    ("kw", 0, 2),
+    ("rw", 5, 2),
+    ("pm", 0, 3),
+    ("pm", 1, 3),
+    ("rw", 0, 3),
+    ("kw", 5, 2),
+    ("pm", 3, 3),
+    ("rc", 7, 1),
+    ("rc", 0, 2),
+    ("kw", 0, 3),
+    ("rw", 7, 3),
+    ("kw", 7, 3),
+    ("rc", 5, 2),
+    ("rw", 5, 3),
+    ("rc", 0, 3),
+    ("kw", 5, 3),
+    ("pm", 0, 0),
+    ("pm", 1, 0),
+    ("pm", 3, 0),
+    ("pm", 2, 0),
+    ("rw", 7, 2),
+    ("pm", 2, 1),
+    ("rc", 7, 3),
+    ("pm", 2, 2),
+    ("kw", 7, 2),
+    ("pm", 2, 3),
     ("pm", 2, 4),
-    ("rw", 3, 3),
-    ("pm", 2, 1),
-    ("rc", 7, 0),
-    ("rd", 0, 0),
-    ("rw", 2, 3),
-    ("wp", 2, 2),
-    ("rc", 3, 1),
-    ("kw", 3, 1),
-    ("ox", 0, 0),
-    ("ry", 3, 1),
-    ("kw", 0, 3),
-    ("pm", 0, 1),
-    ("ko", 5, 0),
-    ("rw", 0, 2),
-    ("rw", 0, 3),
-    ("kw", 5, 1),
-    ("pm", 1, 1),
-    ("rc", 6, 0),
-    ("kw", 3, 3),
-    ("rw", 6, 1),
-    ("rc", 3, 3),
-    ("rc", 2, 1),
-    ("kw", 0, 2),
-    ("ry", 2, 0),
-    ("rc", 0, 1),
-    ("rc", 2, 2),
-    ("kw", 2, 3),
-    ("rc", 2, 3),
-    ("pm", 1, 3),
-    ("rc", 0, 0),
-    ("ko", 6, 0),
-    ("pm", 1, 2),
-    ("pm", 2, 2),
     ("rw", 6, 3),
-    ("rc", 0, 2),
-    ("ry", 3, 0),
-    ("rw", 5, 1),
-    ("pm", 0, 3),
+    ("rc", 5, 3),
     ("kw", 6, 3),
+    ("bw", 0, 0),
     ("rw", 6, 2),
-    ("kw", 6, 1),
-    ("rc", 0, 3),
-    ("pm", 0, 0),
-    ("rc", 6, 3),
-    ("pm", 2, 0),
-    ("rw", 7, 3),
-    ("pm", 0, 2),
-    ("rc", 5, 0),
-    ("pm", 3, 1),
-    ("rc", 6, 1),
-    ("kw", 7, 3),
-    ("rc", 5, 1),
-    ("rw", 7, 2),
-    ("pm", 1, 0),
-    ("pm", 3, 2),
+    ("om", 0, 5),
+    ("om", 1, 5),
+    ("rc", 7, 2),
     ("kw", 6, 2),
-    ("pm", 2, 3),
-    ("rc", 6, 2),
-    ("rw", 5, 2),
-    ("kw", 7, 2),
-    ("pm", 3, 3),
-    ("om", 1, 6),
-    ("om", 0, 6),
-    ("pm", 3, 0),
-    ("kw", 7, 1),
-    ("rw", 5, 3),
-    ("pm", 3, 4),
-    ("rc", 7, 1),
-    ("rc", 7, 2),
-    ("rc", 7, 3),
-    ("om", 0, 7),
-    ("fin", 0, 6),
-    ("rc", 5, 2),
-    ("kw", 5, 3),
-    ("kw", 5, 2),
-    ("fin", 2, 6),
-    ("rc", 5, 3),
-    ("fin", 1, 7),
-    ("om", 1, 7),
-    ("om", 1, 5),
-    ("fin", 3, 6),
-    ("om", 0, 5),
+    ("fin", 0, 5),
+    ("fin", 1, 5),
     ("fin", 2, 5),
     ("fin", 3, 5),
+    ("om", 0, 7),
+    ("rc", 6, 3),
+    ("om", 1, 7),
+    ("rc", 6, 2),
+    ("fin", 0, 7),
+    ("fin", 1, 7),
+    ("fin", 2, 7),
+    ("om", 0, 6),
+    ("om", 1, 6),
     ("fin", 1, 6),
-    ("fin", 0, 5),
-    ("fin", 1, 5),
-    ("fin", 0, 7),
+    ("fin", 0, 6),
+    ("fin", 2, 6),
+    ("fin", 3, 6),
     ("fin", 3, 7),
-    ("fin", 2, 7),
 )
 OUTER = (
+    ("xm", 1, 0),
+    ("xy", 0, 0),
+    ("wd", 4, 0),
+    ("wp", 0, 1),
+    ("ox", 1, 0),
+    ("ox", 2, 0),
+    ("ko", 1, 0),
+    ("ox", 0, 0),
+    ("ko", 2, 0),
+    ("wp", 1, 2),
+    ("wp", 1, 1),
+    ("rc", 2, 0),
+    ("rc", 1, 0),
+    ("ox", 3, 0),
+    ("ko", 0, 0),
     ("xy", 1, 0),
-    ("xm", 1, 0),
+    ("ko", 3, 0),
     ("wp", 4, 2),
-    ("wd", 4, 0),
-    ("xy", 0, 0),
-    ("wd", 1, 0),
-    ("wp", 1, 1),
-    ("bias", 0, 0),
-    ("rw", 1, 2),
-    ("wp", 3, 1),
-    ("ko", 1, 0),
-    ("ox", 1, 0),
+    ("rw", 0, 1),
+    ("rc", 0, 0),
+    ("ox", 4, 0),
+    ("kw", 0, 1),
     ("xf", 1, 0),
-    ("ox", 0, 0),
-    ("wp", 0, 1),
+    ("rc", 3, 0),
+    ("rw", 0, 2),
+    ("ko", 4, 0),
+    ("ry", 1, 0),
+    ("xf", 0, 0),
+    ("rc", 0, 1),
     ("rw", 1, 1),
-    ("rd", 1, 0),
-    ("xf", 0, 0),
-    ("rc", 0, 0),
-    ("ry", 1, 1),
-    ("kw", 1, 3),
-    ("xm", 0, 0),
-    ("rw", 0, 1),
-    ("rw", 1, 3),
-    ("ox", 4, 0),
-    ("wp", 1, 2),
-    ("rc", 1, 2),
-    ("kw", 1, 2),
-    ("rd", 0, 0),
-    ("ry", 1, 0),
-    ("ko", 0, 0),
-    ("rc", 0, 1),
-    ("rc", 1, 0),
-    ("rc", 1, 3),
-    ("wp", 3, 2),
-    ("ko", 4, 0),
-    ("rc", 1, 1),
-    ("rw", 0, 3),
+    ("kw", 0, 2),
+    ("rc", 4, 0),
     ("kw", 1, 1),
     ("ry", 2, 0),
-    ("rw", 0, 2),
+    ("xm", 0, 0),
+    ("ry", 1, 1),
+    ("rc", 0, 2),
+    ("rc", 1, 1),
+    ("rw", 3, 2),
+    ("kw", 3, 2),
+    ("wp", 2, 2),
+    ("rd", 0, 0),
+    ("rc", 3, 2),
+    ("wd", 2, 0),
+    ("rd", 1, 0),
+    ("wp", 3, 2),
+    ("ry", 2, 1),
+    ("rw", 0, 3),
     ("kw", 0, 3),
+    ("wd", 3, 0),
+    ("wd", 1, 0),
+    ("ry", 3, 0),
+    ("rw", 1, 3),
+    ("kw", 1, 3),
+    ("rc", 0, 3),
+    ("rw", 1, 2),
+    ("kw", 1, 2),
+    ("pm", 0, 0),
+    ("pm", 2, 0),
+    ("rc", 1, 3),
+    ("rc", 1, 2),
+    ("ry", 3, 1),
+    ("pm", 1, 0),
     ("pm", 0, 1),
-    ("ry", 2, 1),
+    ("pm", 1, 1),
     ("pm", 2, 1),
-    ("wd", 3, 0),
-    ("ox", 3, 0),
-    ("rc", 0, 2),
+    ("rd", 4, 0),
+    ("rd", 3, 0),
+    ("pm", 3, 0),
+    ("pm", 3, 1),
+    ("we", 7, 0),
+    ("rw", 4, 2),
+    ("kw", 4, 2),
+    ("wp", 3, 1),
+    ("wd", 0, 0),
+    ("rw", 3, 3),
+    ("rw", 4, 3),
+    ("kw", 3, 3),
+    ("wp", 0, 2),
+    ("we", 5, 0),
+    ("wp", 5, 2),
+    ("rc", 4, 2),
+    ("kw", 4, 3),
+    ("re", 7, 0),
+    ("wp", 4, 1),
+    ("rc", 3, 3),
     ("rw", 3, 1),
-    ("ko", 3, 0),
-    ("wp", 2, 2),
-    ("ry", 3, 1),
-    ("kw", 0, 1),
-    ("wd", 2, 0),
-    ("ry", 3, 0),
-    ("rd", 3, 0),
-    ("pm", 1, 1),
+    ("rw", 2, 2),
+    ("kw", 3, 1),
     ("we", 6, 0),
-    ("kw", 0, 2),
-    ("rc", 0, 3),
-    ("pm", 0, 0),
-    ("pm", 1, 0),
-    ("kw", 3, 2),
-    ("wd", 0, 0),
-    ("wp", 0, 2),
-    ("we", 7, 0),
-    ("pm", 3, 0),
-    ("rw", 3, 2),
-    ("kw", 3, 3),
-    ("pm", 3, 1),
-    ("ko", 2, 0),
-    ("ox", 2, 0),
+    ("pw", 1, 1),
+    ("bias", 0, 0),
+    ("rc", 4, 3),
+    ("kw", 2, 2),
+    ("re", 5, 0),
+    ("wp", 7, 2),
+    ("rd", 2, 0),
+    ("rc", 3, 1),
+    ("rw", 4, 1),
+    ("wp", 2, 1),
+    ("om", 0, 3),
+    ("rc", 2, 2),
+    ("om", 1, 3),
     ("re", 6, 0),
-    ("rw", 3, 3),
-    ("rc", 3, 0),
-    ("wp", 2, 1),
+    ("kw", 4, 1),
     ("wp", 6, 2),
-    ("rw", 4, 2),
-    ("wp", 4, 1),
-    ("re", 7, 0),
-    ("rc", 3, 3),
-    ("rc", 3, 1),
-    ("rd", 4, 0),
-    ("kw", 3, 1),
+    ("rw", 2, 3),
+    ("kw", 2, 3),
+    ("rc", 4, 1),
     ("rw", 2, 1),
     ("kw", 2, 1),
-    ("rc", 3, 2),
-    ("om", 0, 3),
-    ("rw", 4, 1),
-    ("wp", 7, 2),
-    ("om", 1, 3),
-    ("rw", 2, 2),
-    ("wp", 5, 2),
-    ("rc", 2, 0),
-    ("rc", 4, 0),
-    ("we", 5, 0),
-    ("kw", 4, 1),
-    ("re", 5, 0),
-    ("rw", 4, 3),
-    ("kw", 4, 2),
-    ("rd", 2, 0),
-    ("rc", 4, 1),
-    ("kw", 4, 3),
-    ("kw", 2, 3),
-    ("rw", 2, 3),
-    ("kw", 2, 2),
-    ("rc", 4, 2),
-    ("rc", 4, 3),
-    ("rc", 2, 2),
-    ("pm", 2, 0),
+    ("om", 0, 4),
+    ("om", 1, 4),
+    ("bw", 0, 0),
+    ("fin", 1, 3),
+    ("fin", 2, 3),
+    ("fin", 0, 3),
+    ("rc", 2, 3),
+    ("fin", 0, 4),
+    ("fin", 1, 4),
+    ("fin", 2, 4),
     ("rc", 2, 1),
-    ("fin", 0, 3),
-    ("om", 0, 4),
-    ("fin", 1, 3),
-    ("om", 1, 4),
-    ("rc", 2, 3),
-    ("fin", 1, 4),
     ("om", 0, 2),
     ("om", 1, 2),
+    ("fin", 0, 2),
     ("fin", 1, 2),
+    ("fin", 2, 2),
     ("fin", 3, 4),
-    ("fin", 2, 2),
-    ("fin", 0, 4),
     ("fin", 3, 2),
     ("fin", 3, 3),
-    ("fin", 2, 3),
-    ("fin", 2, 4),
-    ("fin", 0, 2),
 )
 
 
@@ -407,10 +411,12 @@
 def kernel(
     dims,
     tok_hbm,
+    gain_hbm,
+    w_hbm,
+    bias_hbm,
+    out_ref,
     gain_ref,
-    w_hbm,
     bias_ref,
-    out_ref,
     tok_ref,
     w_ref,
     xsend,
@@ -461,22 +467,40 @@
     pieces = TOKEN_PIECES
     piece_rows = tokens // pieces
 
-    token_load = pltpu.make_async_copy(tok_hbm, tok_ref, load_sem.at[0])
-    weight_load = pltpu.make_async_copy(w_hbm, w_ref, load_sem.at[1])
-    token_load.start()
-    weight_load.start()
+    halves = 2
+    step_rows = tokens // halves
+    row_cut = rows // 2
+
+    def token_load(q):
+        part = pl.ds(q * step_rows, step_rows)
+        return pltpu.make_async_copy(tok_hbm.at[part], tok_ref.at[part], load_sem.at[q])
+
+    def weight_load(q):
+        part = pl.ds(q * row_cut, row_cut)
+        return pltpu.make_async_copy(w_hbm.at[part], w_ref.at[part], load_sem.at[2 + q])
+
+    for q in range(halves):
+        token_load(q).start()
 
     barrier = pltpu.get_barrier_semaphore()
 
-    @pl.loop(1, devices)
-    def _(step):
-        there = lax.rem(flat + step, devices)
-        pl.semaphore_signal(
-            barrier,
-            inc=1,
-            device_id=(there // shard_count, lax.rem(there, shard_count)),
-            device_id_type=MESH,
-        )
+    def greet(owner, there):
+        pl.semaphore_signal(barrier, inc=1, device_id=(owner, there), device_id_type=MESH)
+
+    greet(inst, z_pair * 2 + y)
+    greet(inst, z_mate * 2 + y)
+    greet(inst, z * 2 + 1 - y)
+    greet(x_peer, me)
+    greet(core_peer, me)
+    pl.when(inner)(lambda: greet(inst, z_near * 2 + y))
+    for q in range(2):
+        weight_load(q).start()
+    small_load = (
+        pltpu.make_async_copy(gain_hbm, gain_ref, load_sem.at[4]),
+        pltpu.make_async_copy(bias_hbm, bias_ref, load_sem.at[5]),
+    )
+    for copy in small_load:
+        copy.start()
 
     def remote(source, target, send_sem, recv_sem, device):
         return pltpu.make_async_remote_copy(
@@ -584,30 +608,20 @@
             return TP * query + me * pair + (at - query)
         return TP * (query + pair) + me * pair + (at - query - pair)
 
-    ids = lax.broadcasted_iota(jnp.int32, (rows, rows), 0), lax.broadcasted_iota(jnp.int32, (rows, rows), 1)
-    gain_row = gain_ref[...].astype(jnp.bfloat16).astype(jnp.float32)
-    gain = jnp.sum(jnp.where(ids[0] == ids[1], jnp.broadcast_to(gain_row, (rows, rows)), 0.0), axis=1, keepdims=True)
-    group_id = lax.broadcasted_iota(jnp.int32, (8, held_bias), 0)
-    lane_id = lax.broadcasted_iota(jnp.int32, (8, held_bias), 1)
-    spread = jnp.where(lane_id // group == group_id, jnp.broadcast_to(bias_ref[...], (8, held_bias)), 0.0)
-    from_id = lax.broadcasted_iota(jnp.int32, (held_bias, LANES), 0)
-    to_id = lax.broadcasted_iota(jnp.int32, (held_bias, LANES), 1)
-    pick = jnp.where(lax.rem(from_id, group) == lax.rem(to_id, group), 1.0, 0.0).astype(jnp.bfloat16)
-    bias_own[...] = jnp.dot(spread.astype(jnp.bfloat16), pick, preferred_element_type=jnp.float32)
-
-    token_load.wait()
-    step_rows = 16
-    for first in range(0, tokens, step_rows):
-        values = tok_ref[first : first + step_rows, :].astype(jnp.float32)
+    narrow = 16
+    for first in range(0, tokens, narrow):
+        if first % step_rows == 0:
+            token_load(first // step_rows).wait()
+        values = tok_ref[first : first + narrow, :].astype(jnp.float32)
         mean = jnp.sum(values * values, axis=-1, keepdims=True) * (1.0 / depth)
         scaled = (values * lax.rsqrt(mean + EPSILON)).astype(jnp.bfloat16)
         for which in range(2):
             for owner in range(inst_count):
                 at = (owner * 2 + which) * half_block
-                xsend[which, first : first + step_rows, owner * half_block : (owner + 1) * half_block] = scaled[
+                xsend[which, first : first + narrow, owner * half_block : (owner + 1) * half_block] = scaled[
                     :, at : at + half_block
                 ]
-    pl.semaphore_wait(barrier, devices - 1)
+    pl.semaphore_wait(barrier, jnp.where(inner, 6, 5))
 
     def send_x(name, piece):
         which, device, side = {
@@ -627,7 +641,12 @@
     each(jnp.logical_not(inner), lambda: early(OUTER))
     xbuf[0, half, lax.rem(z, 2)] = xsend[half]
 
-    weight_load.wait()
+    small_load[0].wait()
+    ids = lax.broadcasted_iota(jnp.int32, (rows, rows), 0), lax.broadcasted_iota(jnp.int32, (rows, rows), 1)
+    gain_row = gain_ref[...].astype(jnp.bfloat16).astype(jnp.float32)
+    gain = jnp.sum(jnp.where(ids[0] == ids[1], jnp.broadcast_to(gain_row, (rows, rows)), 0.0), axis=1, keepdims=True)
+    for q in range(2):
+        weight_load(q).wait()
     for rank in range(TP):
         starts = (
             (rank * query, 0, query),
@@ -809,18 +828,20 @@
                 for part in range(2):
                     acc[m, part, first + t] = value[part * 2 * tokens : (part + 1) * 2 * tokens]
 
+        def step_pw(unit, index):
+            side, part = unit // 2, (1 - half if unit % 2 else half)
+            low, extent = incoming(kind)[index]
+            once(
+                ("p", unit, index),
+                lambda: arrived(pbuf.at[side, part, pl.ds(low, extent)], p_recv.at[side, part, index]),
+            )
+
         def step_fin(unit, j):
-            once("bias", finish_bias)
             _, first, count, _ = chunk_of(kind, j)
             side, part = unit // 2, (1 - half if unit % 2 else half)
             for index, (low, extent) in enumerate(incoming(kind)):
                 if low < first + count and first < low + extent:
-                    once(
-                        ("p", unit, index),
-                        lambda: arrived(
-                            pbuf.at[side, part, pl.ds(low, extent)], p_recv.at[side, part, index]
-                        ),
-                    )
+                    step_pw(unit, index)
             where = 1 - y if side else y
             for t in range(first, first + count):
                 value = acc[side, part, t] + pbuf[side, part, t].astype(jnp.float32) + bias_row(column_of(t) // group)
@@ -829,6 +850,14 @@
                     out_ref[part * 2 + k, where, :, t * LANES : (t + 1) * LANES] = value[k * tokens : (k + 1) * tokens]
 
         def step_bias(*_):
+            small_load[1].wait()
+            group_id = lax.broadcasted_iota(jnp.int32, (8, held_bias), 0)
+            lane_id = lax.broadcasted_iota(jnp.int32, (8, held_bias), 1)
+            spread = jnp.where(lane_id // group == group_id, jnp.broadcast_to(bias_ref[...], (8, held_bias)), 0.0)
+            from_id = lax.broadcasted_iota(jnp.int32, (held_bias, LANES), 0)
+            to_id = lax.broadcasted_iota(jnp.int32, (held_bias, LANES), 1)
+            pick = jnp.where(lax.rem(from_id, group) == lax.rem(to_id, group), 1.0, 0.0).astype(jnp.bfloat16)
+            bias_own[...] = jnp.dot(spread.astype(jnp.bfloat16), pick, preferred_element_type=jnp.float32)
             send_bias(False)
 
         table = dict(
@@ -851,6 +880,8 @@
             om=step_om,
             fin=step_fin,
             bias=step_bias,
+            bw=lambda *_: finish_bias(),
+            pw=step_pw,
         )
         start = next(i for i, step in enumerate(steps) if step[0] not in ("xf", "xm", "xy"))
         for name, first, second in steps[start:]:
@@ -898,9 +929,11 @@
     result = pl.pallas_call(
         functools.partial(kernel, dims),
         out_shape=pltpu.VMEM((4, 2, count, tiles * LANES), low),
-        in_specs=[anywhere, vmem, anywhere, vmem],
+        in_specs=[anywhere] * 4,
         out_specs=vmem,
         scratch_shapes=[
+            pltpu.VMEM((1, rows), wide),
+            pltpu.VMEM((1, qkv_bias.shape[0]), wide),
             pltpu.VMEM((count, depth), low),
             pltpu.VMEM((rows, master_qkv.shape[1]), wide),
             pltpu.VMEM((2, count, depth // 2), low),
@@ -914,7 +947,7 @@
             pltpu.VMEM((2, 2, tiles, 2 * count, LANES), wide),
             pltpu.VMEM((8, LANES), wide),
             pltpu.VMEM((devices, 8, LANES), wide),
-            dma((2,)),
+            dma((8,)),
             dma((4, pieces)),
             dma((2,)),
             dma((3,)),

time: 76.7 us -> 75.1 us (0.979)
  Pallas kernels: 75.6 us -> 74 us
    pallas_call x1, Pallas kernels: 75.6 us -> 74 us  [kernel_device(): pl.pallas_call(functools.partial(kernel, dims), out_shape=pltpu.VMEM((4,...]
where the time goes in v5:
time: 75.1 us; the launch traced here: 74.9 us
  Pallas kernels  74 us (99%)
  local copies, waits for them, and re-layouts  0.93 us (1%)
    pallas_call x1, Pallas kernels, kernel_device(): pl.pallas_call(functools.partial(kernel, dims), out_shape=pltpu.VMEM((4,...  74 us

profile of v5, /device:TPU:0, one launch (start us, length us, event | category | flops | bytes accessed | tf_op | source)
XLA Modules:
  0.0 74.9 jit_solution(11011396719478893520)
XLA Ops:
  0.0 74.0 %shard_map.46 = bf16[4,2,64,896]{3,2,1,0:T(8,128)(2,1)S(1)} custom-call(bf16[64,5120]{1,0:T(8,128)(2,1)} %tok_hbm.1, f32[1,160]{1,0:T(1,128)} %bitcast.4, f32[160,7168]{1,0:T(8,128)} %w_hbm.1, f32[1,224]{1,0:T(1,128)} %bitcast.5), custom_call_target="tpu_custom_call" | custom-call | tf_op jit(solution)/shard_map/pallas_call | solution.py:929
  74.0 0.9 %copy.6 = bf16[1,512,896]{2,1,0:T(8,128)(2,1)} copy(bf16[1,512,896]{2,1,0:T(8,128)(2,1)S(1)} %bitcast.3) | data formatting | bytes 1835008

commit v6 on v5

--- a/solution.py
+++ b/solution.py
@@ -23,314 +23,308 @@
 )
 ACROSS = ((5, 6, 7), ())
 INNER = (
+    ("xm", 0, 0),
+    ("xf", 0, 0),
+    ("xf", 1, 0),
+    ("xy", 0, 0),
+    ("wd", 2, 0),
+    ("wp", 0, 1),
+    ("ox", 2, 0),
+    ("ox", 5, 0),
+    ("ko", 2, 0),
+    ("ox", 0, 0),
+    ("xy", 1, 0),
+    ("rc", 2, 0),
+    ("ox", 6, 0),
+    ("ko", 5, 0),
+    ("wp", 0, 2),
+    ("ko", 0, 0),
+    ("wp", 7, 1),
+    ("ko", 6, 0),
+    ("wp", 1, 2),
+    ("rc", 5, 0),
+    ("rw", 0, 1),
+    ("rc", 0, 0),
+    ("ox", 4, 0),
+    ("kw", 0, 1),
+    ("wd", 1, 0),
+    ("ko", 4, 0),
+    ("rw", 4, 2),
+    ("wp", 3, 1),
+    ("rc", 6, 0),
     ("xm", 1, 0),
-    ("xf", 1, 0),
-    ("xf", 0, 0),
-    ("xy", 0, 0),
-    ("wp", 0, 2),
+    ("rc", 0, 1),
+    ("kw", 4, 2),
+    ("rx", 2, 1),
     ("wp", 4, 1),
-    ("ox", 5, 0),
-    ("ox", 2, 0),
-    ("ko", 5, 0),
-    ("ox", 0, 0),
-    ("ko", 2, 0),
-    ("xm", 0, 0),
-    ("rc", 5, 0),
+    ("rc", 4, 0),
+    ("rw", 7, 1),
+    ("kw", 7, 1),
+    ("rd", 4, 0),
+    ("rw", 3, 1),
+    ("wd", 0, 0),
+    ("rc", 4, 2),
+    ("kw", 3, 1),
+    ("rw", 4, 1),
+    ("rc", 7, 1),
+    ("kw", 4, 1),
+    ("ry", 1, 1),
+    ("rx", 2, 0),
+    ("wp", 1, 1),
+    ("rc", 3, 1),
+    ("rw", 4, 3),
+    ("ox", 7, 0),
+    ("kw", 4, 3),
+    ("wp", 2, 1),
+    ("rc", 4, 1),
+    ("rx", 3, 0),
+    ("rw", 1, 2),
+    ("ko", 7, 0),
+    ("ry", 1, 0),
+    ("rc", 4, 3),
+    ("kw", 1, 2),
+    ("rx", 3, 1),
+    ("ry", 3, 1),
+    ("pm", 0, 4),
+    ("rw", 2, 1),
+    ("pm", 1, 4),
+    ("wp", 2, 2),
+    ("rc", 7, 0),
+    ("ox", 3, 0),
+    ("kw", 2, 1),
+    ("rc", 1, 2),
+    ("ko", 3, 0),
+    ("rw", 3, 2),
+    ("pm", 2, 4),
+    ("wd", 3, 0),
+    ("rc", 2, 1),
     ("ox", 1, 0),
-    ("ko", 0, 0),
-    ("ox", 4, 0),
-    ("ko", 1, 0),
-    ("ry", 2, 1),
-    ("rc", 2, 0),
-    ("wp", 1, 1),
-    ("rc", 0, 0),
-    ("ko", 4, 0),
-    ("rw", 4, 1),
-    ("rc", 1, 0),
-    ("rx", 2, 0),
-    ("wd", 1, 0),
-    ("kw", 4, 1),
-    ("rw", 1, 2),
-    ("rd", 4, 0),
-    ("rc", 4, 0),
-    ("ry", 2, 0),
-    ("kw", 1, 2),
-    ("rw", 4, 2),
-    ("wp", 3, 2),
-    ("rc", 4, 1),
-    ("kw", 4, 2),
-    ("wd", 0, 0),
-    ("rc", 1, 2),
-    ("rw", 4, 3),
-    ("rx", 2, 1),
-    ("rw", 1, 1),
-    ("kw", 4, 3),
-    ("ry", 3, 1),
-    ("rc", 4, 2),
-    ("ox", 3, 0),
-    ("kw", 1, 1),
-    ("rx", 3, 0),
-    ("ry", 3, 0),
-    ("rc", 4, 3),
-    ("ox", 6, 0),
-    ("ko", 3, 0),
-    ("wp", 1, 2),
-    ("wp", 6, 1),
-    ("pm", 1, 4),
-    ("rc", 1, 1),
-    ("ox", 7, 0),
-    ("pm", 0, 4),
-    ("rc", 3, 0),
-    ("ko", 6, 0),
-    ("ko", 7, 0),
-    ("rw", 2, 2),
-    ("rx", 3, 1),
-    ("rc", 6, 0),
-    ("rd", 2, 0),
-    ("pm", 3, 4),
-    ("wd", 4, 0),
-    ("wp", 3, 1),
-    ("kw", 2, 2),
-    ("rw", 6, 1),
-    ("wp", 5, 1),
-    ("rc", 7, 0),
-    ("kw", 6, 1),
-    ("wd", 3, 0),
-    ("rc", 2, 2),
-    ("rw", 3, 2),
     ("kw", 3, 2),
     ("rd", 1, 0),
-    ("rw", 3, 1),
-    ("wp", 0, 1),
-    ("rc", 6, 1),
-    ("kw", 3, 1),
     ("wp", 4, 2),
-    ("rw", 5, 1),
+    ("rc", 3, 0),
+    ("rw", 1, 1),
+    ("ko", 1, 0),
     ("rd", 3, 0),
+    ("wp", 3, 2),
     ("rc", 3, 2),
-    ("wp", 2, 2),
-    ("wp", 2, 1),
+    ("kw", 1, 1),
+    ("rd", 2, 0),
     ("rw", 1, 3),
-    ("rc", 3, 1),
+    ("wp", 5, 1),
+    ("rc", 1, 0),
     ("kw", 1, 3),
-    ("rw", 0, 1),
-    ("wp", 7, 1),
-    ("wd", 2, 0),
-    ("rc", 5, 1),
+    ("wd", 4, 0),
+    ("rw", 3, 3),
+    ("wp", 6, 1),
+    ("rc", 1, 1),
+    ("kw", 3, 3),
     ("rw", 2, 3),
-    ("kw", 0, 1),
-    ("ry", 1, 1),
+    ("ry", 2, 0),
+    ("rc", 1, 3),
+    ("rw", 2, 2),
     ("kw", 2, 3),
-    ("rc", 1, 3),
-    ("rw", 2, 1),
-    ("pw", 1, 0),
+    ("pw", 1, 1),
     ("bias", 0, 0),
-    ("rc", 0, 1),
-    ("rw", 3, 3),
-    ("kw", 2, 1),
     ("pm", 0, 1),
     ("pm", 1, 1),
-    ("pm", 3, 1),
+    ("rc", 3, 3),
+    ("kw", 2, 2),
+    ("pm", 2, 1),
+    ("rw", 6, 1),
+    ("pm", 0, 3),
+    ("pm", 1, 3),
     ("rc", 2, 3),
-    ("kw", 3, 3),
-    ("rw", 7, 1),
-    ("rc", 2, 1),
+    ("rw", 5, 1),
+    ("kw", 6, 1),
+    ("pm", 2, 3),
+    ("rd", 0, 0),
+    ("ry", 3, 0),
+    ("rc", 2, 2),
     ("kw", 5, 1),
-    ("kw", 7, 1),
-    ("rd", 0, 0),
-    ("xy", 1, 0),
     ("rw", 0, 2),
-    ("ry", 1, 0),
+    ("ry", 2, 1),
     ("pm", 0, 2),
     ("pm", 1, 2),
-    ("rc", 3, 3),
-    ("pm", 3, 2),
+    ("rc", 6, 1),
     ("kw", 0, 2),
+    ("rw", 0, 3),
+    ("pm", 2, 2),
     ("rw", 5, 2),
-    ("pm", 0, 3),
-    ("pm", 1, 3),
-    ("rw", 0, 3),
+    ("kw", 0, 3),
+    ("rc", 5, 1),
     ("kw", 5, 2),
-    ("pm", 3, 3),
-    ("rc", 7, 1),
+    ("rw", 5, 3),
     ("rc", 0, 2),
-    ("kw", 0, 3),
-    ("rw", 7, 3),
-    ("kw", 7, 3),
-    ("rc", 5, 2),
-    ("rw", 5, 3),
     ("rc", 0, 3),
     ("kw", 5, 3),
     ("pm", 0, 0),
+    ("rw", 7, 2),
     ("pm", 1, 0),
+    ("pm", 2, 0),
+    ("rc", 5, 2),
+    ("kw", 7, 2),
+    ("rc", 5, 3),
     ("pm", 3, 0),
-    ("pm", 2, 0),
-    ("rw", 7, 2),
-    ("pm", 2, 1),
-    ("rc", 7, 3),
-    ("pm", 2, 2),
-    ("kw", 7, 2),
-    ("pm", 2, 3),
-    ("pm", 2, 4),
+    ("rw", 7, 3),
+    ("pm", 3, 1),
+    ("pm", 3, 2),
+    ("kw", 7, 3),
+    ("pm", 3, 3),
+    ("pm", 3, 4),
+    ("rw", 6, 2),
+    ("rc", 7, 2),
+    ("bw", 0, 0),
+    ("om", 1, 5),
+    ("kw", 6, 2),
     ("rw", 6, 3),
-    ("rc", 5, 3),
-    ("kw", 6, 3),
-    ("bw", 0, 0),
-    ("rw", 6, 2),
-    ("om", 0, 5),
-    ("om", 1, 5),
-    ("rc", 7, 2),
-    ("kw", 6, 2),
     ("fin", 0, 5),
     ("fin", 1, 5),
     ("fin", 2, 5),
     ("fin", 3, 5),
-    ("om", 0, 7),
+    ("rc", 7, 3),
+    ("kw", 6, 3),
+    ("rc", 6, 2),
+    ("om", 1, 7),
     ("rc", 6, 3),
-    ("om", 1, 7),
-    ("rc", 6, 2),
     ("fin", 0, 7),
     ("fin", 1, 7),
+    ("fin", 3, 7),
+    ("om", 1, 6),
+    ("fin", 0, 6),
+    ("fin", 1, 6),
+    ("fin", 2, 6),
     ("fin", 2, 7),
-    ("om", 0, 6),
-    ("om", 1, 6),
-    ("fin", 1, 6),
-    ("fin", 0, 6),
-    ("fin", 2, 6),
     ("fin", 3, 6),
-    ("fin", 3, 7),
 )
 OUTER = (
-    ("xm", 1, 0),
-    ("xy", 0, 0),
-    ("wd", 4, 0),
+    ("xm", 0, 0),
+    ("xy", 1, 0),
+    ("wp", 4, 2),
     ("wp", 0, 1),
+    ("ox", 4, 0),
     ("ox", 1, 0),
+    ("ko", 4, 0),
     ("ox", 2, 0),
     ("ko", 1, 0),
+    ("wp", 1, 2),
+    ("rc", 4, 0),
+    ("ox", 3, 0),
+    ("ko", 2, 0),
+    ("ry", 1, 0),
+    ("wp", 1, 1),
+    ("wp", 2, 2),
+    ("rc", 1, 0),
+    ("ko", 3, 0),
+    ("rw", 0, 1),
+    ("wd", 4, 0),
+    ("rc", 2, 0),
+    ("kw", 0, 1),
+    ("rw", 0, 2),
+    ("xy", 0, 0),
+    ("xm", 1, 0),
+    ("rc", 3, 0),
+    ("kw", 0, 2),
+    ("rw", 1, 2),
+    ("rc", 0, 1),
+    ("kw", 1, 2),
+    ("rd", 1, 0),
+    ("rw", 1, 1),
+    ("xf", 0, 0),
+    ("rc", 0, 2),
     ("ox", 0, 0),
-    ("ko", 2, 0),
-    ("wp", 1, 2),
-    ("wp", 1, 1),
-    ("rc", 2, 0),
-    ("rc", 1, 0),
-    ("ox", 3, 0),
+    ("kw", 1, 1),
+    ("rc", 1, 2),
     ("ko", 0, 0),
-    ("xy", 1, 0),
-    ("ko", 3, 0),
-    ("wp", 4, 2),
-    ("rw", 0, 1),
+    ("ry", 1, 1),
+    ("xf", 1, 0),
+    ("rc", 1, 1),
+    ("rw", 1, 3),
+    ("kw", 1, 3),
     ("rc", 0, 0),
-    ("ox", 4, 0),
-    ("kw", 0, 1),
-    ("xf", 1, 0),
-    ("rc", 3, 0),
-    ("rw", 0, 2),
-    ("ko", 4, 0),
-    ("ry", 1, 0),
-    ("xf", 0, 0),
-    ("rc", 0, 1),
-    ("rw", 1, 1),
-    ("kw", 0, 2),
-    ("rc", 4, 0),
-    ("kw", 1, 1),
+    ("ry", 2, 1),
+    ("rc", 1, 3),
+    ("rd", 0, 0),
+    ("pm", 0, 1),
+    ("pm", 2, 1),
+    ("wp", 3, 2),
     ("ry", 2, 0),
-    ("xm", 0, 0),
-    ("ry", 1, 1),
-    ("rc", 0, 2),
-    ("rc", 1, 1),
-    ("rw", 3, 2),
-    ("kw", 3, 2),
-    ("wp", 2, 2),
-    ("rd", 0, 0),
-    ("rc", 3, 2),
-    ("wd", 2, 0),
-    ("rd", 1, 0),
-    ("wp", 3, 2),
-    ("ry", 2, 1),
+    ("wd", 1, 0),
     ("rw", 0, 3),
     ("kw", 0, 3),
     ("wd", 3, 0),
-    ("wd", 1, 0),
     ("ry", 3, 0),
-    ("rw", 1, 3),
-    ("kw", 1, 3),
+    ("wd", 2, 0),
     ("rc", 0, 3),
-    ("rw", 1, 2),
-    ("kw", 1, 2),
     ("pm", 0, 0),
     ("pm", 2, 0),
-    ("rc", 1, 3),
-    ("rc", 1, 2),
     ("ry", 3, 1),
     ("pm", 1, 0),
-    ("pm", 0, 1),
     ("pm", 1, 1),
-    ("pm", 2, 1),
-    ("rd", 4, 0),
+    ("rw", 2, 2),
+    ("kw", 2, 2),
     ("rd", 3, 0),
+    ("wp", 3, 1),
+    ("rc", 2, 2),
     ("pm", 3, 0),
+    ("wp", 2, 1),
     ("pm", 3, 1),
-    ("we", 7, 0),
     ("rw", 4, 2),
     ("kw", 4, 2),
-    ("wp", 3, 1),
+    ("we", 5, 0),
+    ("rw", 3, 2),
     ("wd", 0, 0),
+    ("rw", 3, 1),
+    ("kw", 3, 2),
+    ("wp", 0, 2),
+    ("rc", 4, 2),
+    ("rd", 4, 0),
+    ("rw", 2, 1),
+    ("kw", 3, 1),
+    ("we", 7, 0),
+    ("wp", 5, 2),
+    ("rc", 3, 2),
+    ("re", 5, 0),
     ("rw", 3, 3),
+    ("kw", 2, 1),
+    ("rd", 2, 0),
+    ("wp", 7, 2),
+    ("rc", 3, 1),
+    ("kw", 3, 3),
     ("rw", 4, 3),
-    ("kw", 3, 3),
-    ("wp", 0, 2),
-    ("we", 5, 0),
-    ("wp", 5, 2),
-    ("rc", 4, 2),
+    ("pw", 1, 1),
+    ("bias", 0, 0),
+    ("rc", 2, 1),
     ("kw", 4, 3),
+    ("we", 6, 0),
+    ("rc", 3, 3),
     ("re", 7, 0),
     ("wp", 4, 1),
-    ("rc", 3, 3),
-    ("rw", 3, 1),
-    ("rw", 2, 2),
-    ("kw", 3, 1),
-    ("we", 6, 0),
-    ("pw", 1, 1),
-    ("bias", 0, 0),
-    ("rc", 4, 3),
-    ("kw", 2, 2),
-    ("re", 5, 0),
-    ("wp", 7, 2),
-    ("rd", 2, 0),
-    ("rc", 3, 1),
-    ("rw", 4, 1),
-    ("wp", 2, 1),
-    ("om", 0, 3),
-    ("rc", 2, 2),
-    ("om", 1, 3),
-    ("re", 6, 0),
-    ("kw", 4, 1),
     ("wp", 6, 2),
     ("rw", 2, 3),
     ("kw", 2, 3),
-    ("rc", 4, 1),
-    ("rw", 2, 1),
-    ("kw", 2, 1),
-    ("om", 0, 4),
-    ("om", 1, 4),
+    ("om", 1, 3),
+    ("rc", 4, 3),
+    ("re", 6, 0),
+    ("rc", 2, 3),
+    ("rw", 4, 1),
+    ("kw", 4, 1),
+    ("om", 1, 2),
     ("bw", 0, 0),
     ("fin", 1, 3),
-    ("fin", 2, 3),
     ("fin", 0, 3),
-    ("rc", 2, 3),
+    ("fin", 3, 3),
+    ("fin", 0, 2),
+    ("fin", 1, 2),
+    ("fin", 3, 2),
+    ("rc", 4, 1),
+    ("om", 1, 4),
     ("fin", 0, 4),
     ("fin", 1, 4),
+    ("fin", 2, 2),
+    ("fin", 2, 3),
     ("fin", 2, 4),
-    ("rc", 2, 1),
-    ("om", 0, 2),
-    ("om", 1, 2),
-    ("fin", 0, 2),
-    ("fin", 1, 2),
-    ("fin", 2, 2),
     ("fin", 3, 4),
-    ("fin", 3, 2),
-    ("fin", 3, 3),
 )
 
 
@@ -570,14 +564,21 @@
             result = overlap if result is None else jnp.logical_or(result, overlap)
         return result
 
+    def bias_slot(owner, rank):
+        first = rank * query // held_bias
+        pairs = [(TP * query + (rank + TP * n) * pair) // held_bias for n in range(2)]
+        late = jnp.where(owner - pairs[1] >= 0, 6 + owner - pairs[1], 4 + owner - pairs[0])
+        return jnp.where(jnp.logical_and(owner - first >= 0, owner - first < 4), owner - first, late)
+
     def bias_copy(step):
         there = lax.rem(flat + step, devices)
+        owner, rank = there // shard_count, lax.rem(there, shard_count)
         return remote(
             bias_own,
             bbuf.at[flat],
-            b_send.at[step],
-            b_recv.at[flat],
-            (there // shard_count, lax.rem(there, shard_count)),
+            b_send.at[owner * 3 + lax.rem(rank, 3)],
+            b_recv.at[bias_slot(flat, rank)],
+            (owner, rank),
         )
 
     def send_bias(finish):
@@ -677,7 +678,7 @@
 
             @pl.when(needs(slot, me))
             def _():
-                arrived(bbuf.at[slot], b_recv.at[slot])
+                arrived(bbuf.at[slot], b_recv.at[bias_slot(slot, me)])
 
         bbuf[flat] = bias_own[...]
         send_bias(True)
@@ -818,15 +819,15 @@
                 (inst, (z_pair if what == "far" else z_near) * 2 + y),
             ).start()
 
-        def step_om(m, j):
-            for unit in (0, 1) if m == 0 else (2, 3):
+        def step_om(_, j):
+            for unit in range(4):
                 need_tokens(unit)
             need_chunk(j)
             first = chunk_of(kind, j)[1]
-            lhs = xbuf[m].reshape(4 * tokens, 4 * half_block)
+            lhs = xbuf[...].reshape(8 * tokens, 4 * half_block)
             for t, value in product(kind, lhs, j):
-                for part in range(2):
-                    acc[m, part, first + t] = value[part * 2 * tokens : (part + 1) * 2 * tokens]
+                for unit in range(4):
+                    acc[unit // 2, unit % 2, first + t] = value[unit * 2 * tokens : (unit + 1) * 2 * tokens]
 
         def step_pw(unit, index):
             side, part = unit // 2, (1 - half if unit % 2 else half)
@@ -947,7 +948,7 @@
             pltpu.VMEM((2, 2, tiles, 2 * count, LANES), wide),
             pltpu.VMEM((8, LANES), wide),
             pltpu.VMEM((devices, 8, LANES), wide),
-            dma((8,)),
+            dma((6,)),
             dma((4, pieces)),
             dma((2,)),
             dma((3,)),
@@ -957,10 +958,10 @@
             dma((most,)),
             dma((most,)),
             dma((8,)),
-            dma((2, 2, most)),
+            dma((2, 2, max(len(incoming(way)) for way in range(2)))),
             dma((1,)),
-            dma((devices,)),
-            dma((devices,)),
+            dma((8,)),
+            dma((3 * inst_count,)),
         ],
         compiler_params=pltpu.CompilerParams(
             collective_id=0, has_side_effects=True, vmem_limit_bytes=56 * 1024 * 1024

time: 75.1 us -> 74.5 us (level)
  the two profiles are of different devices: /device:TPU:0 before, /device:TPU:9 now
where the time goes in v6:
time: 74.5 us; the launch traced here: 74.3 us
  Pallas kernels  73.4 us (99%)
  local copies, waits for them, and re-layouts  0.93 us (1%)
    pallas_call x1, Pallas kernels, kernel_device(): pl.pallas_call(functools.partial(kernel, dims), out_shape=pltpu.VMEM((4,...  73.4 us

profile of v6, /device:TPU:9, one launch (start us, length us, event | category | flops | bytes accessed | tf_op | source)
XLA Modules:
  0.0 74.3 jit_solution(6061520125511055058)
XLA Ops:
  0.0 73.4 %shard_map.46 = bf16[4,2,64,896]{3,2,1,0:T(8,128)(2,1)S(1)} custom-call(bf16[64,5120]{1,0:T(8,128)(2,1)} %tok_hbm.1, f32[1,160]{1,0:T(1,128)} %bitcast.4, f32[160,7168]{1,0:T(8,128)} %w_hbm.1, f32[1,224]{1,0:T(1,128)} %bitcast.5), custom_call_target="tpu_custom_call" | custom-call | tf_op jit(solution)/shard_map/pallas_call | solution.py:930
  73.4 0.9 %copy.6 = bf16[1,512,896]{2,1,0:T(8,128)(2,1)} copy(bf16[1,512,896]{2,1,0:T(8,128)(2,1)S(1)} %bitcast.3) | data formatting | bytes 1835008

commit v7 on v6

--- a/solution.py
+++ b/solution.py
@@ -24,306 +24,306 @@
 ACROSS = ((5, 6, 7), ())
 INNER = (
     ("xm", 0, 0),
+    ("xf", 1, 0),
     ("xf", 0, 0),
-    ("xf", 1, 0),
-    ("xy", 0, 0),
-    ("wd", 2, 0),
-    ("wp", 0, 1),
-    ("ox", 2, 0),
-    ("ox", 5, 0),
-    ("ko", 2, 0),
+    ("xy", 1, 0),
+    ("wp", 0, 2),
+    ("wp", 3, 1),
+    ("ox", 7, 0),
     ("ox", 0, 0),
-    ("xy", 1, 0),
-    ("rc", 2, 0),
-    ("ox", 6, 0),
-    ("ko", 5, 0),
-    ("wp", 0, 2),
+    ("ko", 7, 0),
+    ("ox", 3, 0),
     ("ko", 0, 0),
-    ("wp", 7, 1),
-    ("ko", 6, 0),
-    ("wp", 1, 2),
-    ("rc", 5, 0),
-    ("rw", 0, 1),
+    ("wd", 0, 0),
+    ("ox", 1, 0),
+    ("ko", 3, 0),
+    ("rc", 7, 0),
+    ("ry", 2, 1),
+    ("xm", 1, 0),
+    ("ry", 1, 0),
     ("rc", 0, 0),
     ("ox", 4, 0),
-    ("kw", 0, 1),
-    ("wd", 1, 0),
+    ("ko", 1, 0),
+    ("rc", 3, 0),
     ("ko", 4, 0),
     ("rw", 4, 2),
-    ("wp", 3, 1),
+    ("rx", 2, 0),
+    ("rc", 1, 0),
+    ("rw", 3, 1),
+    ("kw", 4, 2),
+    ("rd", 4, 0),
+    ("wp", 3, 2),
+    ("rc", 4, 0),
+    ("wp", 4, 1),
+    ("kw", 3, 1),
+    ("rw", 2, 2),
+    ("wd", 1, 0),
+    ("rc", 4, 2),
+    ("ox", 5, 0),
+    ("kw", 2, 2),
+    ("rx", 2, 1),
+    ("rc", 3, 1),
+    ("ko", 5, 0),
+    ("rw", 4, 3),
+    ("ry", 1, 1),
+    ("wp", 1, 2),
+    ("wp", 5, 1),
+    ("rc", 2, 2),
+    ("kw", 4, 3),
+    ("rw", 4, 1),
+    ("rc", 5, 0),
+    ("rw", 1, 2),
+    ("kw", 4, 1),
+    ("xy", 0, 0),
+    ("rx", 3, 0),
+    ("rc", 4, 3),
+    ("wp", 6, 1),
+    ("kw", 1, 2),
+    ("rw", 5, 1),
+    ("rc", 4, 1),
+    ("ox", 2, 0),
+    ("kw", 5, 1),
+    ("rx", 3, 1),
+    ("wp", 4, 2),
+    ("wp", 2, 1),
+    ("pm", 0, 4),
+    ("rc", 1, 2),
+    ("ox", 6, 0),
+    ("ko", 2, 0),
+    ("pm", 1, 4),
+    ("pm", 2, 4),
+    ("rc", 5, 1),
+    ("ko", 6, 0),
+    ("rd", 3, 0),
+    ("rw", 6, 1),
+    ("wd", 3, 0),
+    ("rd", 0, 0),
+    ("rc", 2, 0),
+    ("kw", 6, 1),
+    ("kw", 2, 1),
+    ("rw", 2, 1),
+    ("rd", 2, 0),
     ("rc", 6, 0),
-    ("xm", 1, 0),
+    ("wp", 2, 2),
+    ("wp", 0, 1),
+    ("rw", 3, 3),
+    ("rc", 6, 1),
+    ("rw", 0, 2),
+    ("kw", 3, 3),
+    ("wd", 2, 0),
+    ("rd", 1, 0),
+    ("wp", 1, 1),
+    ("rc", 2, 1),
+    ("kw", 0, 2),
+    ("rw", 2, 3),
+    ("wd", 4, 0),
+    ("rw", 0, 1),
+    ("wp", 7, 1),
+    ("rc", 3, 3),
+    ("rc", 0, 2),
+    ("kw", 2, 3),
+    ("rw", 0, 3),
+    ("kw", 0, 1),
+    ("ry", 2, 0),
+    ("rw", 1, 3),
+    ("kw", 0, 3),
+    ("pw", 1, 0),
+    ("bias", 0, 0),
+    ("rc", 2, 3),
+    ("kw", 1, 3),
+    ("rw", 1, 1),
     ("rc", 0, 1),
-    ("kw", 4, 2),
-    ("rx", 2, 1),
-    ("wp", 4, 1),
-    ("rc", 4, 0),
+    ("ry", 3, 0),
+    ("pm", 0, 2),
+    ("pm", 1, 2),
+    ("rc", 0, 3),
+    ("kw", 1, 1),
+    ("pm", 2, 2),
     ("rw", 7, 1),
+    ("pm", 0, 0),
+    ("pm", 1, 0),
+    ("rc", 1, 3),
+    ("pm", 2, 0),
     ("kw", 7, 1),
-    ("rd", 4, 0),
-    ("rw", 3, 1),
-    ("wd", 0, 0),
-    ("rc", 4, 2),
-    ("kw", 3, 1),
-    ("rw", 4, 1),
-    ("rc", 7, 1),
-    ("kw", 4, 1),
-    ("ry", 1, 1),
-    ("rx", 2, 0),
-    ("wp", 1, 1),
-    ("rc", 3, 1),
-    ("rw", 4, 3),
-    ("ox", 7, 0),
-    ("kw", 4, 3),
-    ("wp", 2, 1),
-    ("rc", 4, 1),
-    ("rx", 3, 0),
-    ("rw", 1, 2),
-    ("ko", 7, 0),
-    ("ry", 1, 0),
-    ("rc", 4, 3),
-    ("kw", 1, 2),
-    ("rx", 3, 1),
     ("ry", 3, 1),
-    ("pm", 0, 4),
-    ("rw", 2, 1),
-    ("pm", 1, 4),
-    ("wp", 2, 2),
-    ("rc", 7, 0),
-    ("ox", 3, 0),
-    ("kw", 2, 1),
-    ("rc", 1, 2),
-    ("ko", 3, 0),
+    ("rc", 1, 1),
     ("rw", 3, 2),
-    ("pm", 2, 4),
-    ("wd", 3, 0),
-    ("rc", 2, 1),
-    ("ox", 1, 0),
     ("kw", 3, 2),
-    ("rd", 1, 0),
-    ("wp", 4, 2),
-    ("rc", 3, 0),
-    ("rw", 1, 1),
-    ("ko", 1, 0),
-    ("rd", 3, 0),
-    ("wp", 3, 2),
-    ("rc", 3, 2),
-    ("kw", 1, 1),
-    ("rd", 2, 0),
-    ("rw", 1, 3),
-    ("wp", 5, 1),
-    ("rc", 1, 0),
-    ("kw", 1, 3),
-    ("wd", 4, 0),
-    ("rw", 3, 3),
-    ("wp", 6, 1),
-    ("rc", 1, 1),
-    ("kw", 3, 3),
-    ("rw", 2, 3),
-    ("ry", 2, 0),
-    ("rc", 1, 3),
-    ("rw", 2, 2),
-    ("kw", 2, 3),
-    ("pw", 1, 1),
-    ("bias", 0, 0),
     ("pm", 0, 1),
     ("pm", 1, 1),
-    ("rc", 3, 3),
-    ("kw", 2, 2),
     ("pm", 2, 1),
-    ("rw", 6, 1),
+    ("rc", 7, 1),
+    ("rw", 7, 2),
+    ("kw", 7, 2),
+    ("rc", 3, 2),
+    ("rw", 7, 3),
+    ("kw", 7, 3),
     ("pm", 0, 3),
     ("pm", 1, 3),
-    ("rc", 2, 3),
-    ("rw", 5, 1),
-    ("kw", 6, 1),
     ("pm", 2, 3),
-    ("rd", 0, 0),
-    ("ry", 3, 0),
-    ("rc", 2, 2),
-    ("kw", 5, 1),
-    ("rw", 0, 2),
-    ("ry", 2, 1),
-    ("pm", 0, 2),
-    ("pm", 1, 2),
-    ("rc", 6, 1),
-    ("kw", 0, 2),
-    ("rw", 0, 3),
-    ("pm", 2, 2),
-    ("rw", 5, 2),
-    ("kw", 0, 3),
-    ("rc", 5, 1),
-    ("kw", 5, 2),
-    ("rw", 5, 3),
-    ("rc", 0, 2),
-    ("rc", 0, 3),
-    ("kw", 5, 3),
-    ("pm", 0, 0),
-    ("rw", 7, 2),
-    ("pm", 1, 0),
-    ("pm", 2, 0),
-    ("rc", 5, 2),
-    ("kw", 7, 2),
-    ("rc", 5, 3),
+    ("rc", 7, 2),
+    ("rw", 6, 3),
+    ("kw", 6, 3),
     ("pm", 3, 0),
-    ("rw", 7, 3),
     ("pm", 3, 1),
     ("pm", 3, 2),
-    ("kw", 7, 3),
+    ("rw", 6, 2),
     ("pm", 3, 3),
+    ("rc", 7, 3),
+    ("kw", 6, 2),
     ("pm", 3, 4),
-    ("rw", 6, 2),
-    ("rc", 7, 2),
+    ("rw", 5, 2),
     ("bw", 0, 0),
+    ("om", 1, 7),
+    ("rc", 6, 3),
+    ("kw", 5, 2),
+    ("fin", 0, 7),
+    ("rw", 5, 3),
+    ("rc", 6, 2),
+    ("kw", 5, 3),
+    ("fin", 3, 7),
+    ("fin", 1, 7),
+    ("om", 1, 6),
+    ("rc", 5, 2),
+    ("fin", 0, 6),
+    ("fin", 1, 6),
+    ("fin", 2, 6),
+    ("fin", 3, 6),
+    ("rc", 5, 3),
     ("om", 1, 5),
-    ("kw", 6, 2),
-    ("rw", 6, 3),
     ("fin", 0, 5),
     ("fin", 1, 5),
     ("fin", 2, 5),
     ("fin", 3, 5),
-    ("rc", 7, 3),
-    ("kw", 6, 3),
-    ("rc", 6, 2),
-    ("om", 1, 7),
-    ("rc", 6, 3),
-    ("fin", 0, 7),
-    ("fin", 1, 7),
-    ("fin", 3, 7),
-    ("om", 1, 6),
-    ("fin", 0, 6),
-    ("fin", 1, 6),
-    ("fin", 2, 6),
     ("fin", 2, 7),
-    ("fin", 3, 6),
 )
 OUTER = (
     ("xm", 0, 0),
+    ("xy", 0, 0),
+    ("wp", 4, 2),
+    ("wp", 3, 1),
+    ("ox", 3, 0),
+    ("ox", 1, 0),
+    ("ko", 3, 0),
+    ("ox", 0, 0),
+    ("ko", 1, 0),
+    ("wd", 4, 0),
+    ("wp", 0, 1),
+    ("rc", 3, 0),
+    ("ox", 4, 0),
+    ("ko", 0, 0),
     ("xy", 1, 0),
-    ("wp", 4, 2),
-    ("wp", 0, 1),
-    ("ox", 4, 0),
-    ("ox", 1, 0),
+    ("rc", 1, 0),
     ("ko", 4, 0),
+    ("wp", 1, 2),
+    ("rw", 0, 2),
+    ("rc", 0, 0),
+    ("rw", 3, 1),
+    ("kw", 0, 2),
+    ("rd", 0, 0),
+    ("wp", 2, 2),
+    ("rc", 4, 0),
     ("ox", 2, 0),
-    ("ko", 1, 0),
-    ("wp", 1, 2),
-    ("rc", 4, 0),
-    ("ox", 3, 0),
+    ("kw", 3, 1),
+    ("xm", 1, 0),
+    ("rc", 0, 2),
+    ("rw", 0, 1),
     ("ko", 2, 0),
+    ("ry", 1, 1),
+    ("xf", 0, 0),
     ("ry", 1, 0),
+    ("rc", 3, 1),
+    ("kw", 0, 1),
+    ("rw", 0, 3),
+    ("rc", 2, 0),
+    ("kw", 0, 3),
+    ("xf", 1, 0),
     ("wp", 1, 1),
-    ("wp", 2, 2),
-    ("rc", 1, 0),
-    ("ko", 3, 0),
-    ("rw", 0, 1),
-    ("wd", 4, 0),
-    ("rc", 2, 0),
-    ("kw", 0, 1),
-    ("rw", 0, 2),
-    ("xy", 0, 0),
-    ("xm", 1, 0),
-    ("rc", 3, 0),
-    ("kw", 0, 2),
+    ("rw", 3, 2),
+    ("rc", 0, 1),
+    ("kw", 3, 2),
+    ("rc", 0, 3),
+    ("rd", 1, 0),
+    ("pm", 0, 0),
+    ("rc", 3, 2),
+    ("pm", 2, 0),
+    ("ry", 2, 1),
+    ("rw", 1, 1),
+    ("kw", 1, 1),
+    ("ry", 2, 0),
+    ("wd", 3, 0),
+    ("rw", 1, 3),
     ("rw", 1, 2),
-    ("rc", 0, 1),
+    ("kw", 1, 3),
+    ("wd", 0, 0),
+    ("rc", 1, 1),
     ("kw", 1, 2),
-    ("rd", 1, 0),
-    ("rw", 1, 1),
-    ("xf", 0, 0),
-    ("rc", 0, 2),
-    ("ox", 0, 0),
-    ("kw", 1, 1),
+    ("wd", 2, 0),
+    ("rc", 1, 3),
+    ("ry", 3, 0),
+    ("wp", 0, 2),
     ("rc", 1, 2),
-    ("ko", 0, 0),
-    ("ry", 1, 1),
-    ("xf", 1, 0),
-    ("rc", 1, 1),
-    ("rw", 1, 3),
-    ("kw", 1, 3),
-    ("rc", 0, 0),
-    ("ry", 2, 1),
-    ("rc", 1, 3),
-    ("rd", 0, 0),
+    ("wd", 1, 0),
     ("pm", 0, 1),
     ("pm", 2, 1),
-    ("wp", 3, 2),
-    ("ry", 2, 0),
-    ("wd", 1, 0),
-    ("rw", 0, 3),
-    ("kw", 0, 3),
-    ("wd", 3, 0),
-    ("ry", 3, 0),
-    ("wd", 2, 0),
-    ("rc", 0, 3),
-    ("pm", 0, 0),
-    ("pm", 2, 0),
     ("ry", 3, 1),
     ("pm", 1, 0),
     ("pm", 1, 1),
+    ("rw", 4, 2),
+    ("kw", 4, 2),
+    ("rd", 3, 0),
+    ("wp", 2, 1),
     ("rw", 2, 2),
     ("kw", 2, 2),
-    ("rd", 3, 0),
-    ("wp", 3, 1),
+    ("rc", 4, 2),
+    ("pm", 3, 0),
+    ("we", 7, 0),
+    ("pm", 3, 1),
+    ("rw", 3, 3),
+    ("kw", 3, 3),
+    ("wp", 3, 2),
     ("rc", 2, 2),
-    ("pm", 3, 0),
-    ("wp", 2, 1),
-    ("pm", 3, 1),
-    ("rw", 4, 2),
-    ("kw", 4, 2),
-    ("we", 5, 0),
-    ("rw", 3, 2),
-    ("wd", 0, 0),
-    ("rw", 3, 1),
-    ("kw", 3, 2),
-    ("wp", 0, 2),
-    ("rc", 4, 2),
     ("rd", 4, 0),
     ("rw", 2, 1),
-    ("kw", 3, 1),
-    ("we", 7, 0),
-    ("wp", 5, 2),
-    ("rc", 3, 2),
-    ("re", 5, 0),
-    ("rw", 3, 3),
     ("kw", 2, 1),
-    ("rd", 2, 0),
     ("wp", 7, 2),
-    ("rc", 3, 1),
-    ("kw", 3, 3),
-    ("rw", 4, 3),
-    ("pw", 1, 1),
-    ("bias", 0, 0),
-    ("rc", 2, 1),
-    ("kw", 4, 3),
     ("we", 6, 0),
     ("rc", 3, 3),
     ("re", 7, 0),
+    ("om", 1, 3),
+    ("rc", 2, 1),
+    ("rd", 2, 0),
+    ("pw", 1, 2),
+    ("bias", 0, 0),
+    ("rw", 4, 3),
+    ("kw", 4, 3),
     ("wp", 4, 1),
+    ("re", 6, 0),
     ("wp", 6, 2),
+    ("we", 5, 0),
     ("rw", 2, 3),
     ("kw", 2, 3),
-    ("om", 1, 3),
+    ("wp", 5, 2),
     ("rc", 4, 3),
-    ("re", 6, 0),
-    ("rc", 2, 3),
     ("rw", 4, 1),
     ("kw", 4, 1),
+    ("rc", 2, 3),
+    ("re", 5, 0),
     ("om", 1, 2),
     ("bw", 0, 0),
     ("fin", 1, 3),
+    ("fin", 3, 3),
     ("fin", 0, 3),
-    ("fin", 3, 3),
     ("fin", 0, 2),
     ("fin", 1, 2),
     ("fin", 3, 2),
     ("rc", 4, 1),
+    ("fin", 2, 2),
     ("om", 1, 4),
-    ("fin", 0, 4),
     ("fin", 1, 4),
-    ("fin", 2, 2),
     ("fin", 2, 3),
     ("fin", 2, 4),
+    ("fin", 0, 4),
     ("fin", 3, 4),
 )
 

time: 74.5 us -> 73.9 us (level)
  the two profiles are of different devices: /device:TPU:9 before, /device:TPU:0 now
where the time goes in v7:
time: 73.9 us; the launch traced here: 73.3 us
  Pallas kernels  72.4 us (98%)
  local copies, waits for them, and re-layouts  0.93 us (1%)
    pallas_call x1, Pallas kernels, kernel_device(): pl.pallas_call(functools.partial(kernel, dims), out_shape=pltpu.VMEM((4,...  72.4 us

profile of v7, /device:TPU:0, one launch (start us, length us, event | category | flops | bytes accessed | tf_op | source)
XLA Modules:
  0.0 73.3 jit_solution(16465645049502092280)
XLA Ops:
  0.0 72.4 %shard_map.46 = bf16[4,2,64,896]{3,2,1,0:T(8,128)(2,1)S(1)} custom-call(bf16[64,5120]{1,0:T(8,128)(2,1)} %tok_hbm.1, f32[1,160]{1,0:T(1,128)} %bitcast.4, f32[160,7168]{1,0:T(8,128)} %w_hbm.1, f32[1,224]{1,0:T(1,128)} %bitcast.5), custom_call_target="tpu_custom_call" | custom-call | tf_op jit(solution)/shard_map/pallas_call | solution.py:930
  72.4 0.9 %copy.6 = bf16[1,512,896]{2,1,0:T(8,128)(2,1)} copy(bf16[1,512,896]{2,1,0:T(8,128)(2,1)S(1)} %bitcast.3) | data formatting | bytes 1835008
